TPU v7x, 128 devices: a whole 4x4x4 slice. The times are simulated.
128 devices in a mesh: dp: 64 (over z_hi, x, y, core), mp: 2 (over z_lo).
Axes of the slice: x: 4, y: 4, z: 4 (z_hi: 2, z_lo: 2; z = z_hi * 2 + z_lo), core: 2. Of those that a mesh axis runs over, the one named last changes fastest.
Arguments:
- inputs: bfloat16 [8192, 1792], P('dp', 'mp'), may hold values from -6 to 6
- cotangent: bfloat16 [8192, 1792], P('dp', 'mp'), may hold values from -6 to 6
- gate_weight: bfloat16 [9472, 1792], P(('mp', 'dp')), may hold values from -0.125 to 0.125
- up_weight: bfloat16 [9472, 1792], P(('mp', 'dp')), may hold values from -0.125 to 0.125
- down_weight: bfloat16 [9472, 1792], P(('mp', 'dp')), may hold values from -0.0625 to 0.0625
Outputs:
- input_grad: bfloat16 [8192, 1792], P('dp', 'mp')
- gate_grad: bfloat16 [9472, 1792], P(('mp', 'dp'))
All inputs are finite; a program needn't handle non-finite values.
Results may differ from a plain program's by a relative error of at most 0.009.
Values may be sent and summed in bfloat16 or wider, within the bound.
A program may use at most 320 MiB of HBM per device.

v0:
```python
import jax
import jax.numpy as jnp
from jax import lax
from jax.sharding import Mesh
from jax.sharding import PartitionSpec as P

DP = ("dp_0", "dp_1", "dp_2", "dp_3")
MP_DP = ("mp", "dp_0", "dp_1", "dp_2", "dp_3")


def side_by_side(arrays, axis, dim, along):
    widths = [a.shape[along] for a in arrays]
    both = jnp.concatenate(arrays, axis=along)
    filled = lax.all_gather(both, axis, axis=dim, tiled=True)
    return tuple(jnp.split(filled, [sum(widths[:k]) for k in range(1, len(widths))], axis=along))


def split_up(x, dim, peers):
    lengths = x.shape
    pieces = x.reshape(*lengths[:dim], peers, lengths[dim] // peers, *lengths[dim + 1 :])
    return jnp.moveaxis(pieces, dim, 0)


def sent_and_summed(x, axis, dim):
    peers = lax.axis_size(axis)
    pieces = lax.all_to_all(split_up(x, dim, peers), axis, 0, 0, tiled=True)
    return jnp.sum(pieces.astype(jnp.float32), axis=0)


def in_order(pieces, dim):
    pieces = jnp.moveaxis(pieces, 0, dim)
    lengths = pieces.shape
    return pieces.reshape(*lengths[:dim], lengths[dim] * lengths[dim + 1], *lengths[dim + 2 :])


def moved_by_axis(pieces, axes, turns):
    lengths = [lax.axis_size(a) for a in axes]
    pieces = pieces.reshape(*lengths, *pieces.shape[1:])
    for k in turns:
        pieces = lax.all_to_all(pieces, axes[k], split_axis=k, concat_axis=k, tiled=True)
    return pieces.reshape(-1, *pieces.shape[len(axes) :])


def exchange_by_chip(x, groups, turns, split_dim, concat_dim):
    peers = lax.axis_size(groups[0]) * lax.axis_size(groups[1])
    pieces = split_up(x, split_dim, peers)
    return in_order(moved_by_axis(pieces, groups, turns), concat_dim)


def tdot(left, right):
    return lax.dot_general(
        left, right, (((0,), (0,)), ((), ())), preferred_element_type=jnp.float32
    )


def rdot(left, right):
    return lax.dot_general(
        left, right, (((1,), (1,)), ((), ())), preferred_element_type=jnp.float32
    )


def per_device(inputs, cotangent, gate_weight, up_weight, down_weight):
    full_in, full_cot = side_by_side((inputs, cotangent), "mp", 1, 0)
    pieces = lax.all_gather((gate_weight, up_weight), DP, axis=0, tiled=True)
    stacked = jnp.stack([rdot(full_in, pieces[0]), rdot(full_in, pieces[1])])
    gate = stacked[0]
    up = stacked[1]
    dhidden = rdot(full_cot, lax.all_gather(down_weight, DP, axis=0, tiled=True))
    sig = jax.nn.sigmoid(gate)
    act = gate * sig
    dup = (dhidden * act).astype(jnp.bfloat16)
    dgate = (dhidden * up * sig * (1.0 + gate * (1.0 - sig))).astype(jnp.bfloat16)
    owned = exchange_by_chip(dgate, (("dp_0", "dp_1", "dp_2"), "dp_3"), (1, 0), 1, 0)
    gate_sum = tdot(owned, lax.all_gather(full_in, DP, axis=0, tiled=True))
    pieces = (
        lax.all_gather(gate_weight, DP, axis=0, tiled=True),
        lax.all_gather(up_weight, DP, axis=0, tiled=True),
    )
    total = jnp.dot(dgate, pieces[0], preferred_element_type=jnp.float32)
    partial_value = total + jnp.dot(dup, pieces[1], preferred_element_type=jnp.float32)
    input_grad = sent_and_summed(partial_value.astype(jnp.bfloat16), "mp", 1).astype(jnp.bfloat16)
    gate_grad = gate_sum.astype(jnp.bfloat16)
    return (input_grad, gate_grad)


def solution(mesh):
    torus = Mesh(
        mesh.devices.reshape(2, 4, 4, 2, mesh.shape["mp"]), ("dp_0", "dp_1", "dp_2", "dp_3", "mp")
    )
    return jax.shard_map(
        per_device,
        mesh=torus,
        in_specs=(P(DP, "mp"), P(DP, "mp"), P(MP_DP, None), P(MP_DP, None), P(MP_DP, None)),
        out_specs=(P(DP, "mp"), P(MP_DP, None)),
        check_vma=False,
    )
```

profile of v0, /device:TPU:0, one launch (start us, length us, event | category | flops | bytes accessed | tf_op | source)
XLA Modules:
  0.0 529.2 jit_solution(8056646707947620844)
XLA Ops:
  7.2 0.7 all-gather.10.cloned.1.call-update
  7.9 0.7 all-gather.12.cloned.1.call-update
  8.7 0.7 all-gather.14.cloned.1.call-update
  9.4 1.1 pad_maximum_fusion
  10.5 13.2 %all_gather.17 = bf16[256,1792]{1,0:T(8,128)(2,1)S(1)} all-gather(bf16[256,896]{1,0:T(8,128)(2,1)S(1)} %pad_maximum_fusion), channel_id=1, replica_groups=mesh['dp_0'=2,'dp_1'=4,'dp_2'=4,'dp_3'=2,'mp'=2] {'mp'}, dimensions={1}, use_global_device_ids=true | all-gather | bytes 1376256 | tf_op jit(solution)/shard_map/all_gather | solution.py:14
  23.8 0.8 split.9
  24.6 99.6 %all-gather.10.cloned.1.call-done = bf16[64,74,1792]{2,1,0:T(8,128)(2,1)} async-done(((bf16[1,74,1792]{2,1,0:T(8,128)(2,1)}), bf16[64,74,1792]{2,1,0:T(8,128)(2,1)}) %all-gather.10.cloned.1.call-update) | async-done | bytes 16973840 | tf_op jit(solution)/shard_map/all_gather | solution.py:68
  124.2 19.3 %reshape.17 = bf16[4736,1792]{1,0:T(8,128)(2,1)} reshape(bf16[64,74,1792]{2,1,0:T(8,128)(2,1)} %all-gather.10.cloned.1.call-done) | data formatting | bytes 33947648
  143.5 92.0 %all-gather.12.cloned.1.call-done = bf16[64,74,1792]{2,1,0:T(8,128)(2,1)} async-done(((bf16[1,74,1792]{2,1,0:T(8,128)(2,1)}), bf16[64,74,1792]{2,1,0:T(8,128)(2,1)}) %all-gather.12.cloned.1.call-update) | async-done | bytes 16973840 | tf_op jit(solution)/shard_map/all_gather | solution.py:64
  235.5 19.3 %reshape.19 = bf16[4736,1792]{1,0:T(8,128)(2,1)} reshape(bf16[64,74,1792]{2,1,0:T(8,128)(2,1)} %all-gather.12.cloned.1.call-done) | data formatting | bytes 33947648
  254.8 92.0 %all-gather.14.cloned.1.call-done = bf16[64,74,1792]{2,1,0:T(8,128)(2,1)} async-done(((bf16[1,74,1792]{2,1,0:T(8,128)(2,1)}), bf16[64,74,1792]{2,1,0:T(8,128)(2,1)}) %all-gather.14.cloned.1.call-update) | async-done | bytes 16973840 | tf_op jit(solution)/shard_map/all_gather | solution.py:64
  346.8 19.4 %reshape.21 = bf16[4736,1792]{1,0:T(8,128)(2,1)} reshape(bf16[64,74,1792]{2,1,0:T(8,128)(2,1)} %all-gather.14.cloned.1.call-done) | data formatting | bytes 33947648
  366.1 12.8 %fusion.5 = f32[128,4736]{1,0:T(8,128)} fusion(bf16[4736,1792]{1,0:T(8,128)(2,1)} %reshape.17, bf16[256,1792]{1,0:T(8,128)(2,1)S(1)} %all_gather.17), kind=kOutput, calls=%fused_computation.11 | convolution fusion | flops 2172649472 | bytes 19857408 | tf_op jit(solution)/shard_map/dot_general | solution.py:57
  379.0 13.2 %fusion.8 = f32[128,4736]{1,0:T(8,128)} fusion(bf16[4736,1792]{1,0:T(8,128)(2,1)} %reshape.21, bf16[256,1792]{1,0:T(8,128)(2,1)S(1)} %all_gather.17), kind=kOutput, calls=%fused_computation.15 | convolution fusion | flops 2172649472 | bytes 19857408 | tf_op jit(solution)/shard_map/dot_general | solution.py:57
  392.2 13.1 %fusion.2 = bf16[128,4736]{1,0:T(8,128)(2,1)S(1)} fusion(f32[128,4736]{1,0:T(8,128)} %fusion.5, bf16[4736,1792]{1,0:T(8,128)(2,1)} %reshape.19, f32[128,4736]{1,0:T(8,128)} %fusion.8, bf16[256,1792]{1,0:T(8,128)(2,1)S(1)} %all_gather.17), kind=kOutput, calls=%fused_computation.3 | convolution fusion | flops 2178711552 | bytes 23494656 | tf_op jit(solution)/shard_map/dot_general | solution.py:57
  405.3 1.5 copy.10
  406.8 8.4 %fusion.11 = f32[128,1792]{1,0:T(8,128)S(1)} fusion(bf16[128,4736]{1,0:T(8,128)(2,1)S(1)} %fusion.2, bf16[4736,1792]{1,0:T(8,128)(2,1)} %reshape.21), kind=kOutput, calls=%fused_computation.18 | convolution fusion | flops 2172649472 | bytes 19103744 | tf_op jit(solution)/shard_map/dot_general | solution.py:79
  415.2 9.6 %fusion.3 = bf16[128,1792]{1,0:T(8,128)(2,1)S(1)} fusion(f32[128,1792]{1,0:T(8,128)S(1)} %fusion.11, bf16[4736,1792]{1,0:T(8,128)(2,1)} %reshape.19, f32[128,4736]{1,0:T(8,128)S(1)} %copy-done, f32[128,4736]{1,0:T(8,128)S(1)} %copy-done.1), kind=kOutput, calls=%fused_computation.7 | convolution fusion | flops 2176745472 | bytes 23199744 | tf_op jit(solution)/shard_map/dot_general | solution.py:80
  424.9 0.8 copy.16
  425.7 0.3 reshape.14
  426.0 0.5 copy.11
  426.5 4.7 all_to_all.15
  431.2 3.5 all-to-all-start
  434.7 2.4 copy.12
  437.1 11.3 %all-to-all-done = bf16[2,128,896]{2,1,0:T(8,128)(2,1)S(1)} async-done(((bf16[2,128,896]{2,1,0:T(8,128)(2,1)}), bf16[2,128,896]{2,1,0:T(8,128)(2,1)S(1)}, u32[]{:S(2)}, u32[]{:S(2)}) %all-to-all-start) | async-done | bytes 458784 | tf_op jit(solution)/shard_map/all_to_all | solution.py:26
  448.4 7.7 %all-to-all-start.2 = ((bf16[32,2,128,74]{2,1,3,0:T(2,128)(2,1)}), bf16[32,2,128,74]{2,1,3,0:T(2,128)(2,1)S(1)}, u32[]{:S(2)}, u32[]{:S(2)}) async-start(bf16[32,2,128,74]{2,1,3,0:T(2,128)(2,1)} %copy.12), calls=%async_computation.2 | async-start | bytes 2424832 | tf_op jit(solution)/shard_map/all_to_all | solution.py:40
  456.0 0.8 reduce_sum.12
  456.8 18.9 %all-to-all-done.2 = bf16[32,2,128,74]{2,1,3,0:T(2,128)(2,1)S(1)} async-done(((bf16[32,2,128,74]{2,1,3,0:T(2,128)(2,1)}), bf16[32,2,128,74]{2,1,3,0:T(2,128)(2,1)S(1)}, u32[]{:S(2)}, u32[]{:S(2)}) %all-to-all-start.2) | async-done | bytes 1212448 | tf_op jit(solution)/shard_map/all_to_all | solution.py:40
  475.7 1.3 copy.13
  477.0 0.7 reshape_reshape.3
  477.8 32.2 %all-gather.8.cloned.1.call-done = bf16[8192,1792]{1,0:T(8,128)(2,1)} async-done(((bf16[128,1792]{1,0:T(8,128)(2,1)}), bf16[8192,1792]{1,0:T(8,128)(2,1)}) %all-gather.8.cloned.1.call-update) | async-done | bytes 29360144 | tf_op jit(solution)/shard_map/all_gather | solution.py:74
  510.0 12.7 %convolution_convert_fusion = bf16[74,1792]{1,0:T(8,128)(2,1)} fusion(bf16[8192,74]{0,1:T(8,128)(2,1)S(1)} %reshape_reshape.3, bf16[8192,1792]{1,0:T(8,128)(2,1)} %all-gather.8.cloned.1.call-done), kind=kOutput, calls=%fused_computation.8 | convolution fusion | flops 2172782080 | bytes 30837760 | tf_op jit(solution)/shard_map/dot_general | solution.py:51
  (9 shorter events, 0.2 us)
Async XLA Ops:
  7.2 117.0 %all-gather.10.cloned.1.call-start = ((), (), s32[]{:S(2)}) async-start(), calls=%async_computation.4 | async-start | bytes 18636800 | tf_op jit(solution)/shard_map/all_gather | solution.py:68
  7.9 227.6 %all-gather.12.cloned.1.call-start = ((), (), s32[]{:S(2)}) async-start(), calls=%async_computation.5 | async-start | bytes 18636800 | tf_op jit(solution)/shard_map/all_gather | solution.py:64
  8.6 338.1 %all-gather.14.cloned.1.call-start = ((), (), s32[]{:S(2)}) async-start(), calls=%async_computation.6 | async-start | bytes 18636800 | tf_op jit(solution)/shard_map/all_gather | solution.py:64
  9.4 500.6 %all-gather.8.cloned.1.call-start = ((), (), s32[]{:S(2)}) async-start(), calls=%async_computation.3 | async-start | bytes 29818880 | tf_op jit(solution)/shard_map/all_gather | solution.py:74
  406.8 8.4 %copy-start = (f32[128,4736]{1,0:T(8,128)S(1)}, f32[128,4736]{1,0:T(8,128)}, u32[]{:S(2)}) copy-start(f32[128,4736]{1,0:T(8,128)} %fusion.5) | copy-start | bytes 7274500
  406.8 8.4 %copy-start.1 = (f32[128,4736]{1,0:T(8,128)S(1)}, f32[128,4736]{1,0:T(8,128)}, u32[]{:S(2)}) copy-start(f32[128,4736]{1,0:T(8,128)} %fusion.8) | copy-start | bytes 7274500
  431.2 17.1 %all-to-all-start = ((bf16[2,128,896]{2,1,0:T(8,128)(2,1)}), bf16[2,128,896]{2,1,0:T(8,128)(2,1)S(1)}, u32[]{:S(2)}, u32[]{:S(2)}) async-start(bf16[2,128,896]{2,1,0:T(8,128)(2,1)} %bitcast.24), calls=%async_computation | async-start | bytes 917504 | tf_op jit(solution)/shard_map/all_to_all | solution.py:26
  448.4 27.3 %all-to-all-start.2 = ((bf16[32,2,128,74]{2,1,3,0:T(2,128)(2,1)}), bf16[32,2,128,74]{2,1,3,0:T(2,128)(2,1)S(1)}, u32[]{:S(2)}, u32[]{:S(2)}) async-start(bf16[32,2,128,74]{2,1,3,0:T(2,128)(2,1)} %copy.12), calls=%async_computation.2 | async-start | bytes 2424832 | tf_op jit(solution)/shard_map/all_to_all | solution.py:40
Sparse Core Ops, SparseCore 0:
  11.1 113.0 all-gather.9
  127.3 108.1 all-gather.11
  238.6 108.1 all-gather.13
  349.7 160.2 all-gather.7
where the time goes:
time: 532 us; the launch traced here: 529 us
  waiting for transfers between devices  348 us (65%)
  matrix products  69.9 us (13%)
  local copies, waits for them, and re-layouts  66.4 us (12%)
  blocking collectives  17.9 us (3%)
  between operations  13.9 us (3%)
  starting transfers between devices  11.3 us (2%)
    all_gather x2, waiting for transfers between devices, per_device(): pieces = lax.all_gather((gate_weight, up_weight), DP, axis=0, tiled=True)  184 us
    all_gather x1, waiting for transfers between devices, per_device(): lax.all_gather(down_weight, DP, axis=0, tiled=True)  99.6 us
    unnamed x7, local copies, waits for them, and re-layouts  58 us
    dot_general x3, matrix products, rdot(): lax.dot_general(left, right, (((1,), (1,)), ((), ())), preferred_element_...  39.1 us
    all_gather x1, waiting for transfers between devices, per_device(): gate_sum = tdot(owned, lax.all_gather(full_in, DP, axis=0, tiled=True))  32.2 us
    all_to_all x1, waiting for transfers between devices, moved_by_axis(): lax.all_to_all(pieces, axes[k], split_axis=k, concat_axis=k, tiled=True)  18.9 us
    all_gather x1, blocking collectives, side_by_side(): filled = lax.all_gather(both, axis, axis=dim, tiled=True)  13.2 us
    dot_general x1, matrix products, tdot(): lax.dot_general(left, right, (((0,), (0,)), ((), ())), preferred_element_...  12.7 us
  transfers between devices with their start and end apart: 6, of which 6 were waited for; matrix products, arithmetic and copies ran while one was open for 24% of the time, Pallas kernels for 0%

commit v1 on v0

v1 whole, which is shorter than its diff:
```python
import jax
import jax.numpy as jnp
from jax import lax
from jax.sharding import Mesh
from jax.sharding import PartitionSpec as P

DP = ("dp_0", "dp_1", "dp_2", "dp_3")
MP_DP = ("mp", "dp_0", "dp_1", "dp_2", "dp_3")
TOK = ("dp_0", "dp_1", "mp")
HID = ("dp_2", "dp_3")


def tdot(left, right):
    return lax.dot_general(
        left, right, (((0,), (0,)), ((), ())), preferred_element_type=jnp.float32
    )


def rdot(left, right):
    return lax.dot_general(
        left, right, (((1,), (1,)), ((), ())), preferred_element_type=jnp.float32
    )


def whole_rows(pieces):
    groups, rows, width = pieces.shape
    halves = pieces.reshape(groups // 2, 2, rows, width)
    return jnp.moveaxis(halves, 1, 2).reshape(groups // 2 * rows, 2 * width)


def per_device(inputs, cotangent, gate_weight, up_weight, down_weight):
    rows, half = inputs.shape
    full_in = whole_rows(lax.all_gather(inputs, TOK, axis=0))
    full_cot = whole_rows(lax.all_gather(cotangent, TOK, axis=0))
    wg = lax.all_gather(gate_weight, HID, axis=0, tiled=True)
    wu = lax.all_gather(up_weight, HID, axis=0, tiled=True)
    wd = lax.all_gather(down_weight, HID, axis=0, tiled=True)
    gate = rdot(full_in, wg)
    up = rdot(full_in, wu)
    dhidden = rdot(full_cot, wd)
    sig = jax.nn.sigmoid(gate)
    act = gate * sig
    dup = (dhidden * act).astype(jnp.bfloat16)
    dgate = (dhidden * up * sig * (1.0 + gate * (1.0 - sig))).astype(jnp.bfloat16)
    total = jnp.dot(dgate, wg, preferred_element_type=jnp.float32)
    total = total + jnp.dot(dup, wu, preferred_element_type=jnp.float32)
    blocks = total.astype(jnp.bfloat16).reshape(-1, rows, 2, half)
    blocks = jnp.moveaxis(blocks, 2, 1).reshape(-1, rows, half)
    input_grad = lax.psum_scatter(blocks, TOK, scatter_dimension=0)
    gate_sum = tdot(dgate, full_in).astype(jnp.bfloat16)
    gate_grad = lax.psum_scatter(gate_sum, HID, scatter_dimension=0, tiled=True)
    return (input_grad, gate_grad)


def solution(mesh):
    torus = Mesh(
        mesh.devices.reshape(2, 4, 4, 2, mesh.shape["mp"]), ("dp_0", "dp_1", "dp_2", "dp_3", "mp")
    )
    return jax.shard_map(
        per_device,
        mesh=torus,
        in_specs=(P(DP, "mp"), P(DP, "mp"), P(MP_DP, None), P(MP_DP, None), P(MP_DP, None)),
        out_specs=(P(DP, "mp"), P(MP_DP, None)),
        check_vma=False,
    )
```

time: 532 us -> 405 us (0.76)
  matrix products: 69.9 us -> 22.9 us
  waiting for transfers between devices: 348 us -> 305 us
  local copies, waits for them, and re-layouts: 66.4 us -> 35.8 us
  starting transfers between devices: 11.3 us -> 1.53 us
    all_gather x4 -> x5, waiting for transfers between devices: 316 us -> 246 us  [the longest x1 86.1 us: per_device(): full_in = whole_rows(lax.all_gather(inputs, TOK, axis=0))]
    reduce_scatter x0 -> x1, waiting for transfers between devices: none -> 55.8 us  [per_device(): input_grad = lax.psum_scatter(blocks, TOK, scatter_dimension=0)]
    unnamed x7 -> x13, local copies, waits for them, and re-layouts: 58 us -> 10 us
    all_to_all x2 -> x0, waiting for transfers between devices: 30.1 us -> none  [the longest x1 18.9 us: moved_by_axis(): lax.all_to_all(pieces, axes[k], split_axis=k, concat_axis=k, tiled=True)]
    dot_general x3, matrix products: 39.1 us -> 10.5 us  [rdot(): lax.dot_general(left, right, (((1,), (1,)), ((), ())), preferred_element_...]
    unnamed x0 -> x1, blocking collectives: none -> 23 us
    reshape x3, local copies, waits for them, and re-layouts: 1.63 us -> 21.1 us  [the longest x2 13 us: whole_rows(): halves = pieces.reshape(groups // 2, 2, rows, width)]
    all_gather x1 -> x0, blocking collectives: 13.2 us -> none  [side_by_side(): filled = lax.all_gather(both, axis, axis=dim, tiled=True)]
  transfers between devices with their start and end apart: 6 -> 7, of which waited for: 6 -> 6; matrix products, arithmetic and copies ran while one was open for 24% -> 11% of each run, Pallas kernels for 0% -> 0%
where the time goes in v1:
time: 405 us; the launch traced here: 403 us
  waiting for transfers between devices  305 us (75%)
  local copies, waits for them, and re-layouts  35.8 us (9%)
  blocking collectives  23 us (6%)
  matrix products  22.9 us (6%)
  between operations  14.9 us (4%)
    all_gather x1, waiting for transfers between devices, per_device(): full_in = whole_rows(lax.all_gather(inputs, TOK, axis=0))  86.1 us
    all_gather x1, waiting for transfers between devices, per_device(): full_cot = whole_rows(lax.all_gather(cotangent, TOK, axis=0))  82.3 us
    reduce_scatter x1, waiting for transfers between devices, per_device(): input_grad = lax.psum_scatter(blocks, TOK, scatter_dimension=0)  55.8 us
    all_gather x1, waiting for transfers between devices, per_device(): wg = lax.all_gather(gate_weight, HID, axis=0, tiled=True)  27.1 us
    all_gather x1, waiting for transfers between devices, per_device(): wu = lax.all_gather(up_weight, HID, axis=0, tiled=True)  25.8 us
    all_gather x1, waiting for transfers between devices, per_device(): wd = lax.all_gather(down_weight, HID, axis=0, tiled=True)  24.8 us
    unnamed x1, blocking collectives  23 us
    reshape x2, local copies, waits for them, and re-layouts, whole_rows(): halves = pieces.reshape(groups // 2, 2, rows, width)  13 us
  transfers between devices with their start and end apart: 7, of which 6 were waited for; matrix products, arithmetic and copies ran while one was open for 11% of the time, Pallas kernels for 0%

profile of v1, /device:TPU:0, one launch (start us, length us, event | category | flops | bytes accessed | tf_op | source)
XLA Modules:
  0.0 403.2 jit_solution(16914691176496498846)
XLA Ops:
  7.2 0.7 all-gather.19.cloned.1.call-update
  7.9 0.7 all-gather.17.cloned.1.call-update
  8.6 0.0 all-gather.15.cloned.1.call-start
  8.7 0.7 all-gather.15.cloned.1.call-update
  9.4 0.0 all-gather.13.cloned.1.call-start
  9.4 0.5 all-gather.13.cloned.1.call-update
  10.0 0.5 all-gather.11.cloned.1.call-update
  10.5 0.0 reduce-scatter.4.cloned.1.call-start
  10.6 27.1 %all-gather.19.cloned.1.call-done = bf16[8,74,1792]{2,1,0:T(8,128)(2,1)} async-done(((bf16[1,74,1792]{2,1,0:T(8,128)(2,1)}), bf16[8,74,1792]{2,1,0:T(8,128)(2,1)}) %all-gather.19.cloned.1.call-update) | async-done | bytes 2121744 | tf_op jit(solution)/shard_map/all_gather | solution.py:35
  37.7 1.9 reshape.37
  39.6 25.8 %all-gather.17.cloned.1.call-done = bf16[8,74,1792]{2,1,0:T(8,128)(2,1)} async-done(((bf16[1,74,1792]{2,1,0:T(8,128)(2,1)}), bf16[8,74,1792]{2,1,0:T(8,128)(2,1)}) %all-gather.17.cloned.1.call-update) | async-done | bytes 2121744 | tf_op jit(solution)/shard_map/all_gather | solution.py:36
  65.4 2.9 reshape.35
  68.3 24.8 %all-gather.15.cloned.1.call-done = bf16[8,74,1792]{2,1,0:T(8,128)(2,1)} async-done(((bf16[1,74,1792]{2,1,0:T(8,128)(2,1)}), bf16[8,74,1792]{2,1,0:T(8,128)(2,1)}) %all-gather.15.cloned.1.call-update) | async-done | bytes 2121744 | tf_op jit(solution)/shard_map/all_gather | solution.py:37
  93.2 2.9 reshape.33
  96.0 86.1 %all-gather.13.cloned.1.call-done = bf16[2048,896]{1,0:T(8,128)(2,1)} async-done(((bf16[128,896]{1,0:T(8,128)(2,1)}), bf16[2048,896]{1,0:T(8,128)(2,1)}) %all-gather.13.cloned.1.call-update) | async-done | bytes 3670032 | tf_op jit(solution)/shard_map/all_gather | solution.py:33
  182.1 6.5 %copy.12 = bf16[8,2,128,896]{2,0,3,1:T(8,128)(2,1)} copy(bf16[8,2,128,896]{3,2,1,0:T(8,128)(2,1)} %bitcast.44) | data formatting | bytes 7340032 | tf_op jit(solution)/shard_map/reshape | solution.py:27
  188.6 82.3 %all-gather.11.cloned.1.call-done = bf16[2048,896]{1,0:T(8,128)(2,1)} async-done(((bf16[128,896]{1,0:T(8,128)(2,1)}), bf16[2048,896]{1,0:T(8,128)(2,1)}) %all-gather.11.cloned.1.call-update) | async-done | bytes 3670032 | tf_op jit(solution)/shard_map/all_gather | solution.py:34
  271.0 6.5 %copy.11 = bf16[8,2,128,896]{2,0,3,1:T(8,128)(2,1)} copy(bf16[8,2,128,896]{3,2,1,0:T(8,128)(2,1)} %bitcast.48) | data formatting | bytes 7340032 | tf_op jit(solution)/shard_map/reshape | solution.py:27
  277.4 5.2 %fusion.7 = f32[1024,592]{0,1:T(8,128)S(1)} fusion(bf16[592,1792]{1,0:T(8,128)(2,1)} %reshape.33, bf16[224,8,8,128]{3,2,1,0:T(8,128)(2,1)} %bitcast.49), kind=kOutput, calls=%fused_computation.7 | convolution fusion | flops 2172649472 | bytes 8216576 | tf_op jit(solution)/shard_map/dot_general | solution.py:20
  282.6 2.4 fusion.5
  285.0 2.9 multiply_convert_fusion.1
  287.9 3.1 fusion.20
  291.1 4.9 %add_convert_fusion = bf16[1024,1792]{1,0:T(8,128)(2,1)} fusion(f32[1024,1792]{1,0:T(8,128)S(1)} %fusion.20, bf16[592,1792]{1,0:T(8,128)(2,1)S(1)} %copy-done.1, f32[1024,592]{0,1:T(8,128)S(1)} %fusion.7, f32[1024,592]{0,1:T(8,128)S(1)} %fusion.5), kind=kOutput, calls=%fused_computation | convolution fusion | flops 2179956736 | bytes 17981440 | tf_op jit(solution)/shard_map/dot_general | solution.py:46
  296.0 8.1 %reshape.26 = bf16[8,128,2,896]{3,2,1,0:T(2,128)(2,1)} reshape(bf16[1024,1792]{1,0:T(8,128)(2,1)} %add_convert_fusion) | data formatting | bytes 7340032 | tf_op jit(solution)/shard_map/reshape | solution.py:47
  304.1 4.6 %copy.13 = bf16[8,2,128,896]{3,2,1,0:T(8,128)(2,1)} copy(bf16[8,2,128,896]{3,1,2,0:T(2,128)(2,1)} %bitcast.43) | data formatting | bytes 7340032 | tf_op jit(solution)/shard_map/transpose | solution.py:48
  308.7 4.4 %fusion.10 = bf16[592,1792]{1,0:T(8,128)(2,1)S(1)} fusion(bf16[1024,592]{0,1:T(8,128)(2,1)S(1)} %multiply_convert_fusion.1, bf16[224,8,8,128]{3,2,1,0:T(8,128)(2,1)} %bitcast.45), kind=kOutput, calls=%fused_computation.10 | convolution fusion | flops 2173710336 | bytes 7004160 | tf_op jit(solution)/shard_map/dot_general | solution.py:14
  313.2 23.0 %fusion = bf16[80,1792]{1,0:T(8,128)(2,1)S(1)} fusion(bf16[592,1792]{1,0:T(8,128)(2,1)S(1)} %fusion.10), kind=kCustom, calls=%all-reduce-scatter | all-reduce-scatter fusion | flops 1146881 | bytes 2408960
  336.3 1.3 collective-permute-start
  337.6 0.6 dynamic-slice.4
  338.9 0.9 concatenate
  339.8 0.8 constant_dynamic-slice_fusion
  340.6 55.8 %reduce-scatter.4.cloned.1.call-done = bf16[1,128,896]{2,1,0:T(8,128)(2,1)} async-done(((bf16[16,128,896]{2,1,0:T(8,128)(2,1)}), bf16[1,128,896]{2,1,0:T(8,128)(2,1)}) %reduce-scatter.4.cloned.1.call-update) | async-done | bytes 229392 | tf_op jit(solution)/shard_map/reduce_scatter | solution.py:49
  (12 shorter events, 0.2 us)
Async XLA Ops:
  7.2 30.5 %all-gather.19.cloned.1.call-start = ((), (), s32[]{:S(2)}) async-start(), calls=%async_computation.6 | async-start | bytes 2580480 | tf_op jit(solution)/shard_map/all_gather | solution.py:35
  7.9 57.5 %all-gather.17.cloned.1.call-start = ((), (), s32[]{:S(2)}) async-start(), calls=%async_computation.5 | async-start | bytes 2580480 | tf_op jit(solution)/shard_map/all_gather | solution.py:36
  8.6 84.5 %all-gather.15.cloned.1.call-start = ((), (), s32[]{:S(2)}) async-start(), calls=%async_computation.4 | async-start | bytes 2580480 | tf_op jit(solution)/shard_map/all_gather | solution.py:37
  9.4 172.8 %all-gather.13.cloned.1.call-start = ((), (), s32[]{:S(2)}) async-start(), calls=%async_computation.3 | async-start | bytes 3899392 | tf_op jit(solution)/shard_map/all_gather | solution.py:33
  10.0 261.0 %all-gather.11.cloned.1.call-start = ((), (), s32[]{:S(2)}) async-start(), calls=%async_computation.2 | async-start | bytes 3899392 | tf_op jit(solution)/shard_map/all_gather | solution.py:34
  10.5 385.8 %reduce-scatter.4.cloned.1.call-start = ((), (), s32[]{:S(2)}) async-start(), calls=%async_computation.1 | async-start | bytes 3899392 | tf_op jit(solution)/shard_map/reduce_scatter | solution.py:49
  277.4 5.2 %copy-start = (bf16[8,2,128,896]{2,0,3,1:T(8,128)(2,1)S(1)}, bf16[8,2,128,896]{2,0,3,1:T(8,128)(2,1)}, u32[]{:S(2)}) copy-start(bf16[8,2,128,896]{2,0,3,1:T(8,128)(2,1)} %copy.12) | copy-start | bytes 11010052
  282.6 2.4 copy-start.1
  313.2 24.4 %copy-start.2 = (u32[128]{0:T(128)S(1)}, u32[128]{0:T(128)}, u32[]{:S(2)}) copy-start(u32[128]{0:T(128)} %constant.7) | copy-start | bytes 1540
  336.3 2.6 collective-permute-start
Sparse Core Ops, SparseCore 0:
  9.7 28.0 all-gather.18
  39.4 25.9 all-gather.16
  67.1 25.9 all-gather.14
  94.6 87.4 all-gather.12
  183.6 87.2 all-gather.10
  308.9 87.4 reduce-scatter.3

commit v2 on v1

v2 whole, which is shorter than its diff:
```python
import jax
import jax.numpy as jnp
from jax import lax
from jax.experimental import pallas as pl
from jax.experimental.pallas import tpu as pltpu
from jax.sharding import Mesh
from jax.sharding import PartitionSpec as P

DP = ("dp_0", "dp_1", "dp_2", "dp_3")
MP_DP = ("mp", "dp_0", "dp_1", "dp_2", "dp_3")
MESH = pl.DeviceIdType.MESH
F32 = jnp.float32
BF16 = jnp.bfloat16
N = 4
COPIES = 160


def dot(left, right, contract):
    return lax.dot_general(
        left, right, ((contract[:1], contract[1:]), ((), ())), preferred_element_type=F32
    )


class Links:
    def __init__(self, send, recv):
        self.send, self.recv, self.started = send, recv, []

    def copy(self, src, dst, device):
        k = len(self.started)
        c = pltpu.make_async_remote_copy(
            src_ref=src,
            dst_ref=dst,
            send_sem=self.send.at[k],
            recv_sem=self.recv.at[k],
            device_id=device,
            device_id_type=MESH,
        )
        c.start()
        self.started.append(c)
        return c

    def drain(self):
        for c in self.started:
            c.wait_send()


class Place:
    def __init__(self):
        self.x = lax.axis_index("dp_1")
        self.y = lax.axis_index("dp_2")
        self.c = lax.axis_index("dp_3")
        self.z = lax.axis_index("dp_0") * 2 + lax.axis_index("mp")

    def at_z(self, dz):
        z = lax.rem(self.z + (dz + N), N)
        return lax.div(z, 2), lax.rem(z, 2)

    def to(self, axis, step):
        if axis == "x":
            return {"dp_1": lax.rem(self.x + (step + N), N)}
        if axis == "y":
            return {"dp_2": lax.rem(self.y + (step + N), N)}
        if axis == "z":
            high, low = self.at_z(step)
            return {"dp_0": high, "mp": low}
        return {"dp_3": 1 - self.c}


class Tokens:
    def __init__(self, links, place, buf, own, p, q):
        self.links, self.place, self.buf, self.own = links, place, buf, own
        self.p, self.q = p, q
        self.rows, self.half = own.shape
        self.s2, self.f2 = {}, {}

    def slot(self, dx, dz, h):
        high, low = self.place.at_z(dz)
        rows = pl.ds(0, self.rows) if h is None else pl.ds(h * self.rows // 2, self.rows // 2)
        columns = pl.ds(pl.multiple_of(low * self.half, 128), self.half)
        return self.buf.at[dx % N, high, rows, columns]

    def piece(self, kp, kq):
        return (kp, kq) if self.p == "x" else (kq, kp)

    def push(self, kp, kq, h, axis, step):
        dx, dz = self.piece(kp, kq)
        src = self.own if (kp, kq) == (0, 0) else self.slot(dx, dz, h)
        ex = step if axis == "x" else 0
        return self.links.copy(src, self.slot(dx - ex, dz, h), self.place.to(axis, step))

    def start1(self):
        self.s1 = [self.push(0, 0, None, self.p, e) for e in (1, -1)]

    def both2(self, k, h):
        return [self.push(2 if k in ("lo", "hi") else k, 0, h, self.q, e) for e in (1, -1)]

    def start2(self):
        self.s2[0] = self.both2(0, None)

    def after1(self):
        self.s1[0].wait_recv()
        a = self.push(-1, 0, 0, self.p, 1)
        self.s1[1].wait_recv()
        b = self.push(1, 0, 1, self.p, -1)
        self.f1 = [a, b]
        self.s2[-1] = self.both2(-1, None)
        self.s2[1] = self.both2(1, None)

    def after_f1(self):
        self.f1[0].wait_recv()
        self.s2["lo"] = self.both2("lo", 0)
        self.f1[1].wait_recv()
        self.s2["hi"] = self.both2("hi", 1)

    def after2(self, k):
        self.s2[k][0].wait_recv()
        a = self.push(k, -1, 0, self.q, 1)
        self.s2[k][1].wait_recv()
        b = self.push(k, 1, 1, self.q, -1)
        self.f2[k] = [a, b]

    def after2_opposite(self):
        self.s2["lo"][0].wait_recv()
        a = self.push(2, -1, 0, self.q, 1)
        self.s2["hi"][1].wait_recv()
        b = self.push(2, 1, 1, self.q, -1)
        self.s2["lo"][1].wait_recv()
        self.s2["hi"][0].wait_recv()
        self.f2[2] = [a, b]

    def after_f2(self, k):
        for c in self.f2[k]:
            c.wait_recv()


class Weight:
    def __init__(self, links, place, buf, pad):
        self.links, self.place, self.buf, self.pad = links, place, buf, pad
        self.width = buf.shape[1]
        self.core = []

    def slot(self, c, dy, h):
        rows = pl.ds((c * N + dy % N) * self.pad, self.pad)
        if h is None:
            return self.buf.at[rows, :]
        return self.buf.at[rows, pl.ds(h * self.width // 2, self.width // 2)]

    def cross(self, dy, h):
        self.core.append(
            self.links.copy(self.slot(0, dy, h), self.slot(1, dy, h), self.place.to("c", 1))
        )

    def start(self):
        self.s = [
            self.links.copy(self.slot(0, 0, None), self.slot(0, -e, None), self.place.to("y", e))
            for e in (1, -1)
        ]
        self.cross(0, None)

    def after(self):
        self.s[0].wait_recv()
        a = self.links.copy(self.slot(0, -1, 0), self.slot(0, -2, 0), self.place.to("y", 1))
        self.s[1].wait_recv()
        b = self.links.copy(self.slot(0, 1, 1), self.slot(0, 2, 1), self.place.to("y", -1))
        self.f = [a, b]
        self.cross(-1, None)
        self.cross(1, None)

    def after_f(self):
        self.f[0].wait_recv()
        self.cross(2, 0)
        self.f[1].wait_recv()
        self.cross(2, 1)

    def finish(self):
        for c in self.core:
            c.wait_recv()


class Scatter:
    def __init__(self, links, place, axis, mine, send, recv):
        self.links, self.place, self.axis = links, place, axis
        self.mine, self.send, self.recv = mine, send, recv

    def go(self, value, u, h, step):
        self.send[u, h] = value.astype(BF16)
        return self.links.copy(
            self.send.at[u, h], self.recv.at[u, h], self.place.to(self.axis, step)
        )

    def first(self):
        self.a = self.go(self.mine(2, 0), 0, 0, 1)
        self.b = self.go(self.mine(2, 1), 0, 1, -1)

    def direct_right(self):
        self.r1 = self.go(self.mine(1, 1), 1, 1, 1)

    def direct_left(self):
        self.l0 = self.go(self.mine(-1, 0), 2, 0, -1)

    def second(self):
        self.a.wait_recv()
        self.r0 = self.go(self.mine(1, 0) + self.recv[0, 0].astype(F32), 1, 0, 1)
        self.b.wait_recv()
        self.l1 = self.go(self.mine(-1, 1) + self.recv[0, 1].astype(F32), 2, 1, -1)

    def total(self, h):
        (self.r1 if h else self.r0).wait_recv()
        (self.l1 if h else self.l0).wait_recv()
        return self.mine(0, h) + self.recv[1, h].astype(F32) + self.recv[2, h].astype(F32)


def kernel(
    x_ref, y_ref, g_ref, u_ref, d_ref, dx_out, dw_out,
    xb, yb, wb, gate, up, dgate, dup, dx, ra, rb, dwf, dwr,
    a1s, a1r, a2s, a2r, b1s, b1r, b2s, b2r, ws, wr, wcs,
    send_sem, recv_sem, own_sem,
):
    place = Place()
    links = Links(send_sem, recv_sem)
    rows, half = x_ref.shape
    units, width = g_ref.shape
    hidden = wb.shape[1]
    pad = hidden // (2 * N)
    quarter = rows // 4
    block = 2 * rows

    for m, ref in enumerate((g_ref, u_ref, d_ref)):
        if pad > units:
            low = units // 8 * 8
            wb[m, low:pad, :] = jnp.zeros((pad - low, width), BF16)
        wb[m, 0:units, :] = ref[...]
    barrier = pltpu.get_barrier_semaphore()
    peers = [("x", 1), ("x", -1), ("y", 1), ("y", -1), ("z", 1), ("z", -1), ("c", 1)]
    for axis, step in peers:
        pl.semaphore_signal(barrier, inc=1, device_id=place.to(axis, step), device_id_type=MESH)
    pl.semaphore_wait(barrier, len(peers))

    tx = Tokens(links, place, xb, x_ref, "z", "x")
    ty = Tokens(links, place, yb, y_ref, "x", "z")
    wg, wu, wd = (Weight(links, place, wb.at[m], pad) for m in range(3))
    tx.start1()
    ty.start1()
    wg.start()
    tx.start2()
    ty.start2()
    wu.start()
    keep = [
        pltpu.make_async_copy(x_ref, tx.slot(0, 0, None), own_sem.at[0]),
        pltpu.make_async_copy(y_ref, ty.slot(0, 0, None), own_sem.at[1]),
    ]
    for c in keep:
        c.start()
    for c in keep:
        c.wait()

    def tokens_of(buf, k):
        return buf[k % N].reshape(block, width)

    def columns(k):
        return slice(k % N * block, (k % N + 1) * block)

    def forward(out, m, k):
        out[:, columns(k)] = dot(wb[m], tokens_of(xb, k), (1, 1))

    def backward(k):
        dh = dot(wb[2], tokens_of(yb, k), (1, 1))
        g = gate[:, columns(k)]
        sig = jax.nn.sigmoid(g)
        dup[...] = (dh * (g * sig)).astype(BF16)
        dgate[:, columns(k)] = (
            dh * up[:, columns(k)] * sig * (1.0 + g * (1.0 - sig))
        ).astype(BF16)
        part = dot(dgate[:, columns(k)], wb[0], (0, 0)) + dot(dup[...], wb[1], (0, 0))
        dx[k % N] = part.reshape(2, rows, width)

    def z_part(ref, d, start, size):
        high, low = place.at_z(d)
        return ref[high, pl.ds(start, size), pl.ds(pl.multiple_of(low * half, 128), half)]

    a1 = Scatter(links, place, "x", lambda d, h: dx[d % N, h, 0 : rows // 2, :], a1s, a1r)
    a2 = Scatter(
        links, place, "z", lambda d, h: z_part(ra, d, h * quarter, quarter), a2s, a2r
    )
    b1 = [
        Scatter(
            links, place, "z",
            lambda d, h, k=k: z_part(dx.at[k], d, rows // 2 + h * quarter, quarter),
            b1s.at[k], b1r.at[k],
        )
        for k in range(N)
    ]
    b2 = Scatter(
        links, place, "x", lambda d, h: rb[d % N, h * quarter : (h + 1) * quarter, :], b2s, b2r
    )

    def dw_part(d, h):
        r = slice(d % N * pad, (d % N + 1) * pad)
        c = slice(h * half, (h + 1) * half)
        return dwf[r, c] + dwr[r, c].astype(F32)

    w1 = Scatter(links, place, "y", dw_part, ws, wr)

    def b1_start(k):
        b1[k % N].first()
        b1[k % N].direct_right()
        b1[k % N].direct_left()

    def b1_end(k):
        for h in range(2):
            rb[k % N, h * quarter : (h + 1) * quarter, :] = b1[k % N].total(h)

    tx.after1()
    ty.after1()
    wg.after()
    wd.start()
    tx.after2(0)
    ty.after2(0)
    wu.after()
    tx.after_f1()
    ty.after_f1()
    wg.after_f()
    wg.finish()
    forward(gate, 0, 0)
    tx.after2(-1)
    ty.after2(-1)
    wd.after()
    tx.after2(1)
    ty.after2(1)
    wu.after_f()
    wu.finish()
    forward(up, 1, 0)
    tx.after_f2(0)
    ty.after_f2(0)
    wd.after_f()
    wd.finish()
    tx.after2_opposite()
    ty.after2_opposite()
    backward(0)
    b1_start(0)
    for k in (-1, 1):
        forward(gate, 0, k)
        forward(up, 1, k)
        ty.after_f2(k)
        backward(k)
        b1_start(k)
        if k == 1:
            a1.direct_right()
        else:
            a1.direct_left()
    tx.after_f2(-1)
    tx.after_f2(1)
    tx.after_f2(2)
    forward(gate, 0, 2)
    forward(up, 1, 2)
    ty.after_f2(2)
    backward(2)
    a1.first()
    b1_start(2)

    b1[0].second()
    b1[N - 1].second()
    b1[1].second()
    whole = xb[...].reshape(N * block, width)
    other = hidden // 2
    wcs[...] = dot(dgate[other:, :], whole, (1, 0)).astype(BF16)
    cross = links.copy(wcs, dwr, place.to("c", 1))
    a1.second()
    b1[2].second()
    dwf[...] = dot(dgate[0:other, :], whole, (1, 0))
    b1_end(0)
    b1_end(-1)
    b1_end(1)
    cross.wait_recv()
    w1.first()
    w1.direct_right()
    w1.direct_left()
    b2.direct_right()
    b2.direct_left()
    for h in range(2):
        ra[h] = a1.total(h)
    a2.first()
    a2.direct_right()
    a2.direct_left()
    b1_end(2)
    b2.first()
    w1.second()
    a2.second()
    b2.second()
    for h in range(2):
        dw_out[:, h * half : (h + 1) * half] = w1.total(h)[0:units].astype(BF16)
    for h in range(2):
        dx_out[h * quarter : (h + 1) * quarter, :] = a2.total(h).astype(BF16)
    for h in range(2):
        start = rows // 2 + h * quarter
        dx_out[start : start + quarter, :] = b2.total(h).astype(BF16)
    links.drain()


def per_device(inputs, cotangent, gate_weight, up_weight, down_weight):
    rows, half = inputs.shape
    units, width = gate_weight.shape
    pad = -(-units // 16) * 16
    hidden = 2 * N * pad
    tokens = 2 * N * rows
    quarter = rows // 4
    vmem = pltpu.VMEM
    scratch = [
        vmem((N, 2, rows, width), BF16),
        vmem((N, 2, rows, width), BF16),
        vmem((3, hidden, width), BF16),
        vmem((hidden, tokens), F32),
        vmem((hidden, tokens), F32),
        vmem((hidden, tokens), BF16),
        vmem((hidden, 2 * rows), BF16),
        vmem((N, 2, rows, width), F32),
        vmem((2, rows // 2, width), F32),
        vmem((N, rows // 2, half), F32),
        vmem((hidden // 2, width), F32),
        vmem((hidden // 2, width), BF16),
        vmem((3, 2, rows // 2, width), BF16),
        vmem((3, 2, rows // 2, width), BF16),
        vmem((3, 2, quarter, half), BF16),
        vmem((3, 2, quarter, half), BF16),
        vmem((N, 3, 2, quarter, half), BF16),
        vmem((N, 3, 2, quarter, half), BF16),
        vmem((3, 2, quarter, half), BF16),
        vmem((3, 2, quarter, half), BF16),
        vmem((3, 2, pad, half), BF16),
        vmem((3, 2, pad, half), BF16),
        vmem((hidden // 2, width), BF16),
        pltpu.SemaphoreType.DMA((COPIES,)),
        pltpu.SemaphoreType.DMA((COPIES,)),
        pltpu.SemaphoreType.DMA((2,)),
    ]
    return pl.pallas_call(
        kernel,
        out_shape=(
            jax.ShapeDtypeStruct((rows, half), BF16),
            jax.ShapeDtypeStruct((units, width), BF16),
        ),
        in_specs=[pl.BlockSpec(memory_space=vmem)] * 5,
        out_specs=(pl.BlockSpec(memory_space=vmem),) * 2,
        scratch_shapes=scratch,
        compiler_params=pltpu.CompilerParams(
            collective_id=0, has_side_effects=True, vmem_limit_bytes=67043328
        ),
        name="swiglu_grads",
    )(inputs, cotangent, gate_weight, up_weight, down_weight)


def solution(mesh):
    torus = Mesh(
        mesh.devices.reshape(2, 4, 4, 2, mesh.shape["mp"]), ("dp_0", "dp_1", "dp_2", "dp_3", "mp")
    )
    return jax.shard_map(
        per_device,
        mesh=torus,
        in_specs=(P(DP, "mp"), P(DP, "mp"), P(MP_DP, None), P(MP_DP, None), P(MP_DP, None)),
        out_specs=(P(DP, "mp"), P(MP_DP, None)),
        check_vma=False,
    )
```

time: 405 us -> 90.7 us (0.22)
  waiting for transfers between devices: 305 us -> 0 us
  Pallas kernels: 0 us -> 87.5 us
  local copies, waits for them, and re-layouts: 35.8 us -> 2.4 us
  blocking collectives: 23 us -> 0 us
  matrix products: 22.9 us -> 0 us
  between operations: 14.9 us -> 0.65 us
    all_gather x5 -> x0, waiting for transfers between devices: 246 us -> none  [the longest x1 86.1 us: per_device(): full_in = whole_rows(lax.all_gather(inputs, TOK, axis=0))]
    pallas_call x0 -> x1, Pallas kernels: none -> 87.5 us  [per_device(): pl.pallas_call(kernel, out_shape=(jax.ShapeDtypeStruct((rows, half), BF16...]
    reduce_scatter x1 -> x0, waiting for transfers between devices: 55.8 us -> none  [per_device(): input_grad = lax.psum_scatter(blocks, TOK, scatter_dimension=0)]
    unnamed x1 -> x0, blocking collectives: 23 us -> none
    dot_general x6 -> x0, matrix products: 22.9 us -> none  [the longest x3 10.5 us: rdot(): lax.dot_general(left, right, (((1,), (1,)), ((), ())), preferred_element_...]
    reshape x3 -> x0, local copies, waits for them, and re-layouts: 21.1 us -> none  [the longest x2 13 us: whole_rows(): halves = pieces.reshape(groups // 2, 2, rows, width)]
    unnamed x13 -> x4, local copies, waits for them, and re-layouts: 10 us -> 2.4 us
    transpose x1 -> x0, local copies, waits for them, and re-layouts: 4.64 us -> none  [per_device(): blocks = jnp.moveaxis(blocks, 2, 1).reshape(-1, rows, half)]
  transfers between devices with their start and end apart: 7 -> 0, of which waited for: 6 -> 0; matrix products, arithmetic and copies ran while one was open for 11% -> 0% of each run, Pallas kernels for 0% -> 0%
where the time goes in v2:
time: 90.7 us; the launch traced here: 90.6 us
  Pallas kernels  87.5 us (96%)
  local copies, waits for them, and re-layouts  2.4 us (3%)
    pallas_call x1, Pallas kernels, per_device(): pl.pallas_call(kernel, out_shape=(jax.ShapeDtypeStruct((rows, half), BF16...  87.5 us
    unnamed x4, local copies, waits for them, and re-layouts  2.4 us

profile of v2, /device:TPU:0, one launch (start us, length us, event | category | flops | bytes accessed | tf_op | source)
XLA Modules:
  0.0 90.6 jit_solution(2863589846844265256)
XLA Ops:
  0.6 87.5 %swiglu_grads.1 = (bf16[128,896]{1,0:T(8,128)(2,1)}, bf16[74,1792]{1,0:T(8,128)(2,1)}) custom-call(bf16[128,896]{1,0:T(8,128)(2,1)} %x_ref.1, bf16[128,896]{1,0:T(8,128)(2,1)} %y_ref.1, bf16[74,1792]{1,0:T(8,128)(2,1)} %g_ref.1, bf16[74,1792]{1,0:T(8,128)(2,1)} %u_ref.1, bf16[74,1792]{1,0:T(8,128)(2,1)} %d_ref.1), custom_call_target="tpu_custom_call" | custom-call | tf_op jit(solution)/shard_map/swiglu_grads/pallas_call | solution.py:436
  88.2 0.0 copy-start
  88.2 1.7 %copy.9 = bf16[128,896]{1,0:T(8,128)(2,1)} copy(bf16[128,896]{1,0:T(8,128)(2,1)} %get-tuple-element.4) | data formatting | bytes 458752
  89.9 0.0 copy-done
  89.9 0.7 copy.10
Async XLA Ops:
  88.2 1.7 %copy-start = (bf16[74,1792]{1,0:T(8,128)(2,1)S(1)}, bf16[74,1792]{1,0:T(8,128)(2,1)}, u32[]{:S(2)}) copy-start(bf16[74,1792]{1,0:T(8,128)(2,1)} %get-tuple-element.5) | copy-start | bytes 795652

commit v3 on v2

--- a/solution.py
+++ b/solution.py
@@ -12,7 +12,9 @@
 F32 = jnp.float32
 BF16 = jnp.bfloat16
 N = 4
-COPIES = 160
+COPIES = 147
+VMEM_LIMIT = 66400000
+SLOT = (0, 1, 3, 2)
 
 
 def dot(left, right, contract):
@@ -67,26 +69,25 @@
 
 
 class Tokens:
-    def __init__(self, links, place, buf, own, p, q):
-        self.links, self.place, self.buf, self.own = links, place, buf, own
+    def __init__(self, links, place, buf, half, p, q):
+        self.links, self.place, self.buf, self.half = links, place, buf, half
         self.p, self.q = p, q
-        self.rows, self.half = own.shape
+        self.rows = buf.shape[2]
         self.s2, self.f2 = {}, {}
 
     def slot(self, dx, dz, h):
         high, low = self.place.at_z(dz)
         rows = pl.ds(0, self.rows) if h is None else pl.ds(h * self.rows // 2, self.rows // 2)
         columns = pl.ds(pl.multiple_of(low * self.half, 128), self.half)
-        return self.buf.at[dx % N, high, rows, columns]
+        return self.buf.at[SLOT[dx % N], high, rows, columns]
 
     def piece(self, kp, kq):
         return (kp, kq) if self.p == "x" else (kq, kp)
 
     def push(self, kp, kq, h, axis, step):
         dx, dz = self.piece(kp, kq)
-        src = self.own if (kp, kq) == (0, 0) else self.slot(dx, dz, h)
         ex = step if axis == "x" else 0
-        return self.links.copy(src, self.slot(dx - ex, dz, h), self.place.to(axis, step))
+        return self.links.copy(self.slot(dx, dz, h), self.slot(dx - ex, dz, h), self.place.to(axis, step))
 
     def start1(self):
         self.s1 = [self.push(0, 0, None, self.p, e) for e in (1, -1)]
@@ -98,11 +99,13 @@
         self.s2[0] = self.both2(0, None)
 
     def after1(self):
-        self.s1[0].wait_recv()
-        a = self.push(-1, 0, 0, self.p, 1)
-        self.s1[1].wait_recv()
-        b = self.push(1, 0, 1, self.p, -1)
-        self.f1 = [a, b]
+        for c in self.s1:
+            c.wait_recv()
+
+    def forward1(self):
+        self.f1 = [self.push(-1, 0, 0, self.p, 1), self.push(1, 0, 1, self.p, -1)]
+
+    def spread1(self):
         self.s2[-1] = self.both2(-1, None)
         self.s2[1] = self.both2(1, None)
 
@@ -150,11 +153,11 @@
             self.links.copy(self.slot(0, dy, h), self.slot(1, dy, h), self.place.to("c", 1))
         )
 
+    def turn(self, h, step):
+        return self.links.copy(self.slot(0, 0, h), self.slot(0, -step, h), self.place.to("y", step))
+
     def start(self):
-        self.s = [
-            self.links.copy(self.slot(0, 0, None), self.slot(0, -e, None), self.place.to("y", e))
-            for e in (1, -1)
-        ]
+        self.s = [self.turn(0, 1), self.turn(1, -1), self.turn(1, 1), self.turn(0, -1)]
         self.cross(0, None)
 
     def after(self):
@@ -163,7 +166,11 @@
         self.s[1].wait_recv()
         b = self.links.copy(self.slot(0, 1, 1), self.slot(0, 2, 1), self.place.to("y", -1))
         self.f = [a, b]
+
+    def after_rest(self):
+        self.s[2].wait_recv()
         self.cross(-1, None)
+        self.s[3].wait_recv()
         self.cross(1, None)
 
     def after_f(self):
@@ -212,7 +219,7 @@
 
 def kernel(
     x_ref, y_ref, g_ref, u_ref, d_ref, dx_out, dw_out,
-    xb, yb, wb, gate, up, dgate, dup, dx, ra, rb, dwf, dwr,
+    xb, yb, wb, win, gu, dgu, dgate, dx, ra, rb, dwf, dwr,
     a1s, a1r, a2s, a2r, b1s, b1r, b2s, b2r, ws, wr, wcs,
     send_sem, recv_sem, own_sem,
 ):
@@ -225,74 +232,84 @@
     quarter = rows // 4
     block = 2 * rows
 
-    for m, ref in enumerate((g_ref, u_ref, d_ref)):
-        if pad > units:
-            low = units // 8 * 8
-            wb[m, low:pad, :] = jnp.zeros((pad - low, width), BF16)
-        wb[m, 0:units, :] = ref[...]
     barrier = pltpu.get_barrier_semaphore()
     peers = [("x", 1), ("x", -1), ("y", 1), ("y", -1), ("z", 1), ("z", -1), ("c", 1)]
     for axis, step in peers:
         pl.semaphore_signal(barrier, inc=1, device_id=place.to(axis, step), device_id_type=MESH)
+    tx = Tokens(links, place, xb, half, "z", "x")
+    ty = Tokens(links, place, yb, half, "x", "z")
+    wg, wu, wd = (Weight(links, place, wb.at[m], pad) for m in range(3))
+    pairs = [(x_ref, tx.slot(0, 0, None)), (y_ref, ty.slot(0, 0, None))]
+    pairs += [(ref, win.at[m]) for m, ref in enumerate((g_ref, u_ref, d_ref))]
+    loads = [pltpu.make_async_copy(a, b, own_sem.at[k]) for k, (a, b) in enumerate(pairs)]
+    for c in loads:
+        c.start()
+
+    def place_weight(m):
+        loads[2 + m].wait()
+        if pad > units:
+            low = units // 8 * 8
+            wb[m, low:pad, :] = jnp.zeros((pad - low, width), BF16)
+        wb[m, 0:units, :] = win[m]
+
+    for c in loads[:2]:
+        c.wait()
     pl.semaphore_wait(barrier, len(peers))
-
-    tx = Tokens(links, place, xb, x_ref, "z", "x")
-    ty = Tokens(links, place, yb, y_ref, "x", "z")
-    wg, wu, wd = (Weight(links, place, wb.at[m], pad) for m in range(3))
     tx.start1()
     ty.start1()
-    wg.start()
     tx.start2()
     ty.start2()
+    place_weight(0)
+    wg.start()
+    place_weight(1)
     wu.start()
-    keep = [
-        pltpu.make_async_copy(x_ref, tx.slot(0, 0, None), own_sem.at[0]),
-        pltpu.make_async_copy(y_ref, ty.slot(0, 0, None), own_sem.at[1]),
+    place_weight(2)
+
+    def spot(k):
+        return SLOT[k % N]
+
+    def forward(k, count):
+        a = spot(k)
+        tokens = xb[a : a + count].reshape(count * block, width)
+        both = dot(tokens, wb[0:2].reshape(2 * hidden, width), (1, 1))
+        gu[a : a + count] = both.reshape(count, block, 2 * hidden)
+
+    def backward(k):
+        a = spot(k)
+        dh = dot(yb[a].reshape(block, width), wb[2], (1, 1))
+        g = gu[a, :, 0:hidden]
+        sig = jax.nn.sigmoid(g)
+        dg = (dh * gu[a, :, hidden:] * sig * (1.0 + g * (1.0 - sig))).astype(BF16)
+        dgu[:, 0:hidden] = dg
+        dgu[:, hidden:] = (dh * (g * sig)).astype(BF16)
+        part = dot(dgu[...], wb[0:2].reshape(2 * hidden, width), (1, 0))
+        dx[a] = part.reshape(2, rows, width)
+        dgate[:, a * block : (a + 1) * block] = dgu[:, 0:hidden].T
+
+    def z_part(k, d, start):
+        high, low = place.at_z(d)
+        columns = pl.ds(pl.multiple_of(low * half, 128), half)
+        return dx[spot(k), high, pl.ds(start, quarter), columns]
+
+    def quarters(h):
+        return slice(h * quarter, (h + 1) * quarter)
+
+    a1 = [
+        Scatter(
+            links, place, "x", lambda d, h, j=j: z_part(d, j, h * quarter), a1s.at[j], a1r.at[j]
+        )
+        for j in range(N)
     ]
-    for c in keep:
-        c.start()
-    for c in keep:
-        c.wait()
-
-    def tokens_of(buf, k):
-        return buf[k % N].reshape(block, width)
-
-    def columns(k):
-        return slice(k % N * block, (k % N + 1) * block)
-
-    def forward(out, m, k):
-        out[:, columns(k)] = dot(wb[m], tokens_of(xb, k), (1, 1))
-
-    def backward(k):
-        dh = dot(wb[2], tokens_of(yb, k), (1, 1))
-        g = gate[:, columns(k)]
-        sig = jax.nn.sigmoid(g)
-        dup[...] = (dh * (g * sig)).astype(BF16)
-        dgate[:, columns(k)] = (
-            dh * up[:, columns(k)] * sig * (1.0 + g * (1.0 - sig))
-        ).astype(BF16)
-        part = dot(dgate[:, columns(k)], wb[0], (0, 0)) + dot(dup[...], wb[1], (0, 0))
-        dx[k % N] = part.reshape(2, rows, width)
-
-    def z_part(ref, d, start, size):
-        high, low = place.at_z(d)
-        return ref[high, pl.ds(start, size), pl.ds(pl.multiple_of(low * half, 128), half)]
-
-    a1 = Scatter(links, place, "x", lambda d, h: dx[d % N, h, 0 : rows // 2, :], a1s, a1r)
-    a2 = Scatter(
-        links, place, "z", lambda d, h: z_part(ra, d, h * quarter, quarter), a2s, a2r
-    )
+    a2 = Scatter(links, place, "z", lambda d, h: ra[d % N, quarters(h), :], a2s, a2r)
     b1 = [
         Scatter(
             links, place, "z",
-            lambda d, h, k=k: z_part(dx.at[k], d, rows // 2 + h * quarter, quarter),
+            lambda d, h, k=k: z_part(k, d, rows // 2 + h * quarter),
             b1s.at[k], b1r.at[k],
         )
         for k in range(N)
     ]
-    b2 = Scatter(
-        links, place, "x", lambda d, h: rb[d % N, h * quarter : (h + 1) * quarter, :], b2s, b2r
-    )
+    b2 = Scatter(links, place, "x", lambda d, h: rb[d % N, quarters(h), :], b2s, b2r)
 
     def dw_part(d, h):
         r = slice(d % N * pad, (d % N + 1) * pad)
@@ -300,100 +317,113 @@
         return dwf[r, c] + dwr[r, c].astype(F32)
 
     w1 = Scatter(links, place, "y", dw_part, ws, wr)
+    order = (2, 1, 3, 0)
 
     def b1_start(k):
         b1[k % N].first()
         b1[k % N].direct_right()
         b1[k % N].direct_left()
 
-    def b1_end(k):
+    def end(stage, out, k):
         for h in range(2):
-            rb[k % N, h * quarter : (h + 1) * quarter, :] = b1[k % N].total(h)
+            out[k % N, quarters(h), :] = stage[k % N].total(h)
 
     tx.after1()
     ty.after1()
+    tx.forward1()
+    tx.spread1()
+    ty.spread1()
     wg.after()
+    wg.after_rest()
+    wu.after()
     wd.start()
+    tx.after_f1()
+    ty.forward1()
     tx.after2(0)
     ty.after2(0)
-    wu.after()
-    tx.after_f1()
-    ty.after_f1()
+    wu.after_rest()
     wg.after_f()
-    wg.finish()
-    forward(gate, 0, 0)
     tx.after2(-1)
     ty.after2(-1)
-    wd.after()
+    wu.after_f()
+    wg.finish()
+    wu.finish()
+    forward(0, 1)
     tx.after2(1)
     ty.after2(1)
-    wu.after_f()
-    wu.finish()
-    forward(up, 1, 0)
-    tx.after_f2(0)
+    wd.after()
+    tx.after2_opposite()
+    wd.after_rest()
+    forward(1, 1)
+    ty.after_f1()
+    wd.after_f()
+    forward(-1, 1)
+    wd.finish()
+    ty.after_f2(-1)
+    backward(-1)
+    b1_start(-1)
+    for j in order:
+        a1[j].direct_left()
+    ty.after2_opposite()
+    ty.after_f2(1)
+    backward(1)
+    b1_start(1)
+    for j in order:
+        a1[j].direct_right()
     ty.after_f2(0)
-    wd.after_f()
-    wd.finish()
-    tx.after2_opposite()
-    ty.after2_opposite()
     backward(0)
     b1_start(0)
-    for k in (-1, 1):
-        forward(gate, 0, k)
-        forward(up, 1, k)
-        ty.after_f2(k)
-        backward(k)
-        b1_start(k)
-        if k == 1:
-            a1.direct_right()
-        else:
-            a1.direct_left()
+    tx.after_f2(0)
     tx.after_f2(-1)
     tx.after_f2(1)
     tx.after_f2(2)
-    forward(gate, 0, 2)
-    forward(up, 1, 2)
+    forward(2, 1)
+    b1[N - 1].second()
+    b1[1].second()
     ty.after_f2(2)
     backward(2)
-    a1.first()
+    for j in order:
+        a1[j].first()
     b1_start(2)
 
-    b1[0].second()
-    b1[N - 1].second()
-    b1[1].second()
     whole = xb[...].reshape(N * block, width)
     other = hidden // 2
     wcs[...] = dot(dgate[other:, :], whole, (1, 0)).astype(BF16)
     cross = links.copy(wcs, dwr, place.to("c", 1))
-    a1.second()
+    b1[0].second()
     b1[2].second()
+    a1[2].second()
+    a1[1].second()
     dwf[...] = dot(dgate[0:other, :], whole, (1, 0))
-    b1_end(0)
-    b1_end(-1)
-    b1_end(1)
+    a1[3].second()
+    a1[0].second()
     cross.wait_recv()
     w1.first()
+    end(b1, rb, 2)
+    b2.first()
+    end(a1, ra, 2)
+    a2.first()
+    end(b1, rb, 3)
+    b2.direct_left()
+    end(b1, rb, 1)
+    b2.direct_right()
+    end(a1, ra, 1)
+    a2.direct_right()
+    end(a1, ra, 3)
+    a2.direct_left()
     w1.direct_right()
     w1.direct_left()
-    b2.direct_right()
-    b2.direct_left()
+    b2.second()
+    a2.second()
+    end(b1, rb, 0)
+    end(a1, ra, 0)
+    w1.second()
     for h in range(2):
-        ra[h] = a1.total(h)
-    a2.first()
-    a2.direct_right()
-    a2.direct_left()
-    b1_end(2)
-    b2.first()
-    w1.second()
-    a2.second()
-    b2.second()
+        dx_out[quarters(2 + h), :] = b2.total(h).astype(BF16)
+    for h in range(2):
+        dx_out[quarters(h), :] = a2.total(h).astype(BF16)
     for h in range(2):
         dw_out[:, h * half : (h + 1) * half] = w1.total(h)[0:units].astype(BF16)
-    for h in range(2):
-        dx_out[h * quarter : (h + 1) * quarter, :] = a2.total(h).astype(BF16)
-    for h in range(2):
-        start = rows // 2 + h * quarter
-        dx_out[start : start + quarter, :] = b2.total(h).astype(BF16)
     links.drain()
 
 
@@ -405,33 +435,34 @@
     tokens = 2 * N * rows
     quarter = rows // 4
     vmem = pltpu.VMEM
+    ring = (3, 2, quarter, half)
     scratch = [
         vmem((N, 2, rows, width), BF16),
         vmem((N, 2, rows, width), BF16),
         vmem((3, hidden, width), BF16),
-        vmem((hidden, tokens), F32),
-        vmem((hidden, tokens), F32),
+        vmem((3, units, width), BF16),
+        vmem((N, 2 * rows, 2 * hidden), F32),
+        vmem((2 * rows, 2 * hidden), BF16),
         vmem((hidden, tokens), BF16),
-        vmem((hidden, 2 * rows), BF16),
         vmem((N, 2, rows, width), F32),
-        vmem((2, rows // 2, width), F32),
+        vmem((N, rows // 2, half), F32),
         vmem((N, rows // 2, half), F32),
         vmem((hidden // 2, width), F32),
         vmem((hidden // 2, width), BF16),
-        vmem((3, 2, rows // 2, width), BF16),
-        vmem((3, 2, rows // 2, width), BF16),
-        vmem((3, 2, quarter, half), BF16),
-        vmem((3, 2, quarter, half), BF16),
-        vmem((N, 3, 2, quarter, half), BF16),
-        vmem((N, 3, 2, quarter, half), BF16),
-        vmem((3, 2, quarter, half), BF16),
-        vmem((3, 2, quarter, half), BF16),
+        vmem((N,) + ring, BF16),
+        vmem((N,) + ring, BF16),
+        vmem(ring, BF16),
+        vmem(ring, BF16),
+        vmem((N,) + ring, BF16),
+        vmem((N,) + ring, BF16),
+        vmem(ring, BF16),
+        vmem(ring, BF16),
         vmem((3, 2, pad, half), BF16),
         vmem((3, 2, pad, half), BF16),
         vmem((hidden // 2, width), BF16),
         pltpu.SemaphoreType.DMA((COPIES,)),
         pltpu.SemaphoreType.DMA((COPIES,)),
-        pltpu.SemaphoreType.DMA((2,)),
+        pltpu.SemaphoreType.DMA((5,)),
     ]
     return pl.pallas_call(
         kernel,
@@ -439,11 +470,11 @@
             jax.ShapeDtypeStruct((rows, half), BF16),
             jax.ShapeDtypeStruct((units, width), BF16),
         ),
-        in_specs=[pl.BlockSpec(memory_space=vmem)] * 5,
+        in_specs=[pl.BlockSpec(memory_space=pltpu.HBM)] * 5,
         out_specs=(pl.BlockSpec(memory_space=vmem),) * 2,
         scratch_shapes=scratch,
         compiler_params=pltpu.CompilerParams(
-            collective_id=0, has_side_effects=True, vmem_limit_bytes=67043328
+            collective_id=0, has_side_effects=True, vmem_limit_bytes=VMEM_LIMIT
         ),
         name="swiglu_grads",
     )(inputs, cotangent, gate_weight, up_weight, down_weight)

time: 90.7 us -> 78.5 us (0.87)
  Pallas kernels: 87.5 us -> 75.3 us
    pallas_call x1, Pallas kernels: 87.5 us -> 75.3 us  [per_device(): pl.pallas_call(kernel, out_shape=(jax.ShapeDtypeStruct((rows, half), BF16...]
where the time goes in v3:
time: 78.5 us; the launch traced here: 78.4 us
  Pallas kernels  75.3 us (96%)
  local copies, waits for them, and re-layouts  2.4 us (3%)
    pallas_call x1, Pallas kernels, per_device(): pl.pallas_call(kernel, out_shape=(jax.ShapeDtypeStruct((rows, half), BF16...  75.3 us
    unnamed x4, local copies, waits for them, and re-layouts  2.4 us

profile of v3, /device:TPU:0, one launch (start us, length us, event | category | flops | bytes accessed | tf_op | source)
XLA Modules:
  0.0 78.4 jit_solution(11734450906106022942)
XLA Ops:
  0.6 75.3 %swiglu_grads.1 = (bf16[128,896]{1,0:T(8,128)(2,1)}, bf16[74,1792]{1,0:T(8,128)(2,1)}) custom-call(bf16[128,896]{1,0:T(8,128)(2,1)} %x_ref.1, bf16[128,896]{1,0:T(8,128)(2,1)} %y_ref.1, bf16[74,1792]{1,0:T(8,128)(2,1)} %g_ref.1, bf16[74,1792]{1,0:T(8,128)(2,1)} %u_ref.1, bf16[74,1792]{1,0:T(8,128)(2,1)} %d_ref.1), custom_call_target="tpu_custom_call" | custom-call | tf_op jit(solution)/shard_map/swiglu_grads/pallas_call | solution.py:467
  76.0 0.0 copy-start
  76.0 1.7 %copy.9 = bf16[128,896]{1,0:T(8,128)(2,1)} copy(bf16[128,896]{1,0:T(8,128)(2,1)} %get-tuple-element.4) | data formatting | bytes 458752
  77.7 0.0 copy-done
  77.7 0.7 copy.10
Async XLA Ops:
  76.0 1.7 %copy-start = (bf16[74,1792]{1,0:T(8,128)(2,1)S(1)}, bf16[74,1792]{1,0:T(8,128)(2,1)}, u32[]{:S(2)}) copy-start(bf16[74,1792]{1,0:T(8,128)(2,1)} %get-tuple-element.5) | copy-start | bytes 795652

commit v4 on v3

--- a/solution.py
+++ b/solution.py
@@ -1,3 +1,5 @@
+import math
+
 import jax
 import jax.numpy as jnp
 from jax import lax
@@ -12,7 +14,7 @@
 F32 = jnp.float32
 BF16 = jnp.bfloat16
 N = 4
-COPIES = 147
+GROUPS = 58
 VMEM_LIMIT = 66400000
 SLOT = (0, 1, 3, 2)
 
@@ -23,27 +25,41 @@
     )
 
 
+class Group:
+    def __init__(self, sem):
+        self.sem = sem
+
+    def wait(self, like):
+        pltpu.make_async_copy(like, like, self.sem).wait()
+
+
 class Links:
-    def __init__(self, send, recv):
-        self.send, self.recv, self.started = send, recv, []
-
-    def copy(self, src, dst, device):
-        k = len(self.started)
-        c = pltpu.make_async_remote_copy(
+    def __init__(self, send, recv, limits):
+        self.send, self.recv, self.limits = send, recv, limits
+        self.groups = 0
+        self.sent = [0] * len(limits)
+
+    def group(self):
+        self.groups += 1
+        return Group(self.recv.at[self.groups - 1])
+
+    def copy(self, src, dst, device, group, kinds=(0,)):
+        size = math.prod(src.shape) * src.dtype.itemsize
+        kind = next(k for k in kinds if self.sent[k] + size <= self.limits[k])
+        self.sent[kind] += size
+        pltpu.make_async_remote_copy(
             src_ref=src,
             dst_ref=dst,
-            send_sem=self.send.at[k],
-            recv_sem=self.recv.at[k],
+            send_sem=self.send.at[kind],
+            recv_sem=group.sem,
             device_id=device,
             device_id_type=MESH,
-        )
-        c.start()
-        self.started.append(c)
-        return c
-
-    def drain(self):
-        for c in self.started:
-            c.wait_send()
+        ).start()
+
+    def drain(self, refs):
+        assert self.sent == self.limits, self.sent
+        for k, ref in enumerate(refs):
+            pltpu.make_async_copy(ref, ref, self.send.at[k]).wait()
 
 
 class Place:
@@ -84,63 +100,73 @@
     def piece(self, kp, kq):
         return (kp, kq) if self.p == "x" else (kq, kp)
 
-    def push(self, kp, kq, h, axis, step):
+    def push(self, kp, kq, h, axis, step, group):
         dx, dz = self.piece(kp, kq)
         ex = step if axis == "x" else 0
-        return self.links.copy(self.slot(dx, dz, h), self.slot(dx - ex, dz, h), self.place.to(axis, step))
+        self.links.copy(
+            self.slot(dx, dz, h), self.slot(dx - ex, dz, h), self.place.to(axis, step), group
+        )
+
+    def pair(self, kp, kq, h, axis):
+        group = self.links.group()
+        for e in (1, -1):
+            self.push(kp, kq, h, axis, e, group)
+        return group
+
+    def onward(self, pieces, axis):
+        group = self.links.group()
+        for (kp, kq), h, e in zip(pieces, (0, 1), (1, -1)):
+            self.push(kp, kq, h, axis, e, group)
+        return group
+
+    def one(self):
+        return self.buf.at[0, 0, :, 0 : self.half]
+
+    def two(self):
+        return self.buf.at[0, 0]
 
     def start1(self):
-        self.s1 = [self.push(0, 0, None, self.p, e) for e in (1, -1)]
-
-    def both2(self, k, h):
-        return [self.push(2 if k in ("lo", "hi") else k, 0, h, self.q, e) for e in (1, -1)]
+        self.s1 = self.pair(0, 0, None, self.p)
 
     def start2(self):
-        self.s2[0] = self.both2(0, None)
+        self.s2[0] = self.pair(0, 0, None, self.q)
 
     def after1(self):
-        for c in self.s1:
-            c.wait_recv()
+        self.s1.wait(self.two())
 
     def forward1(self):
-        self.f1 = [self.push(-1, 0, 0, self.p, 1), self.push(1, 0, 1, self.p, -1)]
+        self.f1 = self.onward(((-1, 0), (1, 0)), self.p)
 
     def spread1(self):
-        self.s2[-1] = self.both2(-1, None)
-        self.s2[1] = self.both2(1, None)
+        self.s2[-1] = self.pair(-1, 0, None, self.q)
+        self.s2[1] = self.pair(1, 0, None, self.q)
 
     def after_f1(self):
-        self.f1[0].wait_recv()
-        self.s2["lo"] = self.both2("lo", 0)
-        self.f1[1].wait_recv()
-        self.s2["hi"] = self.both2("hi", 1)
+        self.f1.wait(self.one())
+        self.near = self.onward(((2, 0), (2, 0)), self.q)
+        self.far = self.links.group()
+        self.push(2, 0, 1, self.q, 1, self.far)
+        self.push(2, 0, 0, self.q, -1, self.far)
 
     def after2(self, k):
-        self.s2[k][0].wait_recv()
-        a = self.push(k, -1, 0, self.q, 1)
-        self.s2[k][1].wait_recv()
-        b = self.push(k, 1, 1, self.q, -1)
-        self.f2[k] = [a, b]
+        self.s2[k].wait(self.two())
+        self.f2[k] = self.onward(((k, -1), (k, 1)), self.q)
 
     def after2_opposite(self):
-        self.s2["lo"][0].wait_recv()
-        a = self.push(2, -1, 0, self.q, 1)
-        self.s2["hi"][1].wait_recv()
-        b = self.push(2, 1, 1, self.q, -1)
-        self.s2["lo"][1].wait_recv()
-        self.s2["hi"][0].wait_recv()
-        self.f2[2] = [a, b]
+        self.near.wait(self.one())
+        self.f2[2] = self.onward(((2, -1), (2, 1)), self.q)
+
+    def after2_rest(self):
+        self.far.wait(self.one())
 
     def after_f2(self, k):
-        for c in self.f2[k]:
-            c.wait_recv()
+        self.f2[k].wait(self.one())
 
 
 class Weight:
     def __init__(self, links, place, buf, pad):
         self.links, self.place, self.buf, self.pad = links, place, buf, pad
         self.width = buf.shape[1]
-        self.core = []
 
     def slot(self, c, dy, h):
         rows = pl.ds((c * N + dy % N) * self.pad, self.pad)
@@ -148,73 +174,81 @@
             return self.buf.at[rows, :]
         return self.buf.at[rows, pl.ds(h * self.width // 2, self.width // 2)]
 
-    def cross(self, dy, h):
-        self.core.append(
-            self.links.copy(self.slot(0, dy, h), self.slot(1, dy, h), self.place.to("c", 1))
+    def cross(self, dy):
+        self.links.copy(
+            self.slot(0, dy, None), self.slot(1, dy, None), self.place.to("c", 1), self.core, (1,)
         )
 
-    def turn(self, h, step):
-        return self.links.copy(self.slot(0, 0, h), self.slot(0, -step, h), self.place.to("y", step))
+    def turn(self, dy, h, step, group):
+        self.links.copy(
+            self.slot(0, dy, h), self.slot(0, dy - step, h), self.place.to("y", step), group, (1,)
+        )
+
+    def one(self):
+        return self.buf.at[0 : self.pad]
 
     def start(self):
-        self.s = [self.turn(0, 1), self.turn(1, -1), self.turn(1, 1), self.turn(0, -1)]
-        self.cross(0, None)
+        self.near, self.far, self.core = (self.links.group() for _ in range(3))
+        self.turn(0, 0, 1, self.near)
+        self.turn(0, 1, -1, self.near)
+        self.turn(0, 1, 1, self.far)
+        self.turn(0, 0, -1, self.far)
+        self.cross(0)
 
     def after(self):
-        self.s[0].wait_recv()
-        a = self.links.copy(self.slot(0, -1, 0), self.slot(0, -2, 0), self.place.to("y", 1))
-        self.s[1].wait_recv()
-        b = self.links.copy(self.slot(0, 1, 1), self.slot(0, 2, 1), self.place.to("y", -1))
-        self.f = [a, b]
+        self.near.wait(self.one())
+        self.last = self.links.group()
+        self.turn(-1, 0, 1, self.last)
+        self.turn(1, 1, -1, self.last)
 
     def after_rest(self):
-        self.s[2].wait_recv()
-        self.cross(-1, None)
-        self.s[3].wait_recv()
-        self.cross(1, None)
+        self.far.wait(self.one())
+        self.cross(-1)
+        self.cross(1)
 
     def after_f(self):
-        self.f[0].wait_recv()
-        self.cross(2, 0)
-        self.f[1].wait_recv()
-        self.cross(2, 1)
+        self.last.wait(self.one())
+        self.cross(2)
 
     def finish(self):
-        for c in self.core:
-            c.wait_recv()
+        self.core.wait(self.buf.at[0 : N * self.pad])
 
 
 class Scatter:
-    def __init__(self, links, place, axis, mine, send, recv):
+    def __init__(self, links, place, axis, mine, send, recv, like, kinds=(2,)):
+        self.kinds = kinds
         self.links, self.place, self.axis = links, place, axis
-        self.mine, self.send, self.recv = mine, send, recv
-
-    def go(self, value, u, h, step):
+        self.mine, self.send, self.recv, self.like = mine, send, recv, like
+        self.early, self.late = links.group(), links.group()
+
+    def go(self, value, u, h, step, group):
         self.send[u, h] = value.astype(BF16)
-        return self.links.copy(
-            self.send.at[u, h], self.recv.at[u, h], self.place.to(self.axis, step)
+        self.links.copy(
+            self.send.at[u, h], self.recv.at[u, h], self.place.to(self.axis, step), group,
+            self.kinds,
         )
 
     def first(self):
-        self.a = self.go(self.mine(2, 0), 0, 0, 1)
-        self.b = self.go(self.mine(2, 1), 0, 1, -1)
+        self.go(self.mine(2, 0), 0, 0, 1, self.early)
+        self.go(self.mine(2, 1), 0, 1, -1, self.early)
 
     def direct_right(self):
-        self.r1 = self.go(self.mine(1, 1), 1, 1, 1)
+        self.go(self.mine(1, 1), 1, 1, 1, self.late)
 
     def direct_left(self):
-        self.l0 = self.go(self.mine(-1, 0), 2, 0, -1)
+        self.go(self.mine(-1, 0), 2, 0, -1, self.late)
 
     def second(self):
-        self.a.wait_recv()
-        self.r0 = self.go(self.mine(1, 0) + self.recv[0, 0].astype(F32), 1, 0, 1)
-        self.b.wait_recv()
-        self.l1 = self.go(self.mine(-1, 1) + self.recv[0, 1].astype(F32), 2, 1, -1)
-
-    def total(self, h):
-        (self.r1 if h else self.r0).wait_recv()
-        (self.l1 if h else self.l0).wait_recv()
-        return self.mine(0, h) + self.recv[1, h].astype(F32) + self.recv[2, h].astype(F32)
+        self.early.wait(self.like[0])
+        self.go(self.mine(1, 0) + self.recv[0, 0].astype(F32), 1, 0, 1, self.late)
+        self.go(self.mine(-1, 1) + self.recv[0, 1].astype(F32), 2, 1, -1, self.late)
+
+    def totals(self):
+        self.late.wait(self.like[1])
+        return [
+            self.mine(0, h) + self.recv[1, h].astype(F32) + self.recv[2, h].astype(F32)
+            for h in range(2)
+        ]
 
 
 def kernel(
@@ -224,7 +258,8 @@
     send_sem, recv_sem, own_sem,
 ):
     place = Place()
-    links = Links(send_sem, recv_sem)
+    whole_bytes = math.prod(dx.shape) * 4
+    links = Links(send_sem, recv_sem, [whole_bytes, whole_bytes, whole_bytes // 2])
     rows, half = x_ref.shape
     units, width = g_ref.shape
     hidden = wb.shape[1]
@@ -294,29 +329,33 @@
     def quarters(h):
         return slice(h * quarter, (h + 1) * quarter)
 
+    like = (xb.at[0, 0, 0 : rows // 2, 0:half], xb.at[0, 0, :, 0:half])
+    spare = (0, 1, 2)
     a1 = [
         Scatter(
-            links, place, "x", lambda d, h, j=j: z_part(d, j, h * quarter), a1s.at[j], a1r.at[j]
+            links, place, "x", lambda d, h, j=j: z_part(d, j, h * quarter),
+            a1s.at[j], a1r.at[j], like,
         )
         for j in range(N)
     ]
-    a2 = Scatter(links, place, "z", lambda d, h: ra[d % N, quarters(h), :], a2s, a2r)
+    a2 = Scatter(links, place, "z", lambda d, h: ra[d % N, quarters(h), :], a2s, a2r, like, spare)
     b1 = [
         Scatter(
             links, place, "z",
             lambda d, h, k=k: z_part(k, d, rows // 2 + h * quarter),
-            b1s.at[k], b1r.at[k],
+            b1s.at[k], b1r.at[k], like,
         )
         for k in range(N)
     ]
-    b2 = Scatter(links, place, "x", lambda d, h: rb[d % N, quarters(h), :], b2s, b2r)
+    b2 = Scatter(links, place, "x", lambda d, h: rb[d % N, quarters(h), :], b2s, b2r, like, spare)
 
     def dw_part(d, h):
         r = slice(d % N * pad, (d % N + 1) * pad)
         c = slice(h * half, (h + 1) * half)
         return dwf[r, c] + dwr[r, c].astype(F32)
 
-    w1 = Scatter(links, place, "y", dw_part, ws, wr)
+    like_w = (wb.at[0, 0:pad], wb.at[0, 0 : 2 * pad])
+    w1 = Scatter(links, place, "y", dw_part, ws, wr, like_w)
     order = (2, 1, 3, 0)
 
     def b1_start(k):
@@ -325,8 +364,8 @@
         b1[k % N].direct_left()
 
     def end(stage, out, k):
-        for h in range(2):
-            out[k % N, quarters(h), :] = stage[k % N].total(h)
+        for h, total in enumerate(stage[k % N].totals()):
+            out[k % N, quarters(h), :] = total
 
     tx.after1()
     ty.after1()
@@ -353,6 +392,7 @@
     ty.after2(1)
     wd.after()
     tx.after2_opposite()
+    tx.after2_rest()
     wd.after_rest()
     forward(1, 1)
     ty.after_f1()
@@ -361,70 +401,81 @@
     wd.finish()
     ty.after_f2(-1)
     backward(-1)
-    b1_start(-1)
-    for j in order:
-        a1[j].direct_left()
     ty.after2_opposite()
     ty.after_f2(1)
     backward(1)
+    for j in order:
+        a1[j].direct_left()
+        a1[j].direct_right()
+    b1_start(-1)
     b1_start(1)
-    for j in order:
-        a1[j].direct_right()
     ty.after_f2(0)
     backward(0)
-    b1_start(0)
+    b1[0].first()
     tx.after_f2(0)
     tx.after_f2(-1)
     tx.after_f2(1)
     tx.after_f2(2)
     forward(2, 1)
     b1[N - 1].second()
-    b1[1].second()
+    ty.after2_rest()
     ty.after_f2(2)
     backward(2)
     for j in order:
         a1[j].first()
-    b1_start(2)
+    b1[2].first()
+    b1[1].second()
 
     whole = xb[...].reshape(N * block, width)
     other = hidden // 2
-    wcs[...] = dot(dgate[other:, :], whole, (1, 0)).astype(BF16)
-    cross = links.copy(wcs, dwr, place.to("c", 1))
-    b1[0].second()
+    upper = slice(other // 2, other)
+    lower = slice(0, other // 2)
+    crossings = []
+    for part in (upper, lower):
+        wcs[part] = dot(dgate[other + part.start : other + part.stop], whole, (1, 0)).astype(BF16)
+        crossings.append(links.group())
+        links.copy(wcs.at[part], dwr.at[part], place.to("c", 1), crossings[-1], (1,))
+    b1[2].direct_right()
+    b1[2].direct_left()
+    dwf[upper] = dot(dgate[upper], whole, (1, 0))
     b1[2].second()
+    crossings[0].wait(dwr.at[upper])
+    w1.first()
+    dwf[lower] = dot(dgate[lower], whole, (1, 0))
     a1[2].second()
     a1[1].second()
-    dwf[...] = dot(dgate[0:other, :], whole, (1, 0))
     a1[3].second()
     a1[0].second()
-    cross.wait_recv()
-    w1.first()
     end(b1, rb, 2)
     b2.first()
-    end(a1, ra, 2)
-    a2.first()
+    crossings[1].wait(dwr.at[lower])
+    w1.direct_right()
+    w1.direct_left()
+    b1[0].second()
+    b1[0].direct_right()
+    b1[0].direct_left()
     end(b1, rb, 3)
     b2.direct_left()
     end(b1, rb, 1)
     b2.direct_right()
+    w1.second()
+    end(a1, ra, 2)
+    a2.first()
     end(a1, ra, 1)
     a2.direct_right()
     end(a1, ra, 3)
     a2.direct_left()
-    w1.direct_right()
-    w1.direct_left()
     b2.second()
+    end(b1, rb, 0)
     a2.second()
-    end(b1, rb, 0)
     end(a1, ra, 0)
-    w1.second()
-    for h in range(2):
-        dx_out[quarters(2 + h), :] = b2.total(h).astype(BF16)
-    for h in range(2):
-        dx_out[quarters(h), :] = a2.total(h).astype(BF16)
-    for h in range(2):
-        dw_out[:, h * half : (h + 1) * half] = w1.total(h)[0:units].astype(BF16)
-    links.drain()
+    for h, total in enumerate(b2.totals()):
+        dx_out[quarters(2 + h), :] = total.astype(BF16)
+    for h, total in enumerate(a2.totals()):
+        dx_out[quarters(h), :] = total.astype(BF16)
+    for h, total in enumerate(w1.totals()):
+        dw_out[:, h * half : (h + 1) * half] = total[0:units].astype(BF16)
+    links.drain((dx, dx, xb))
 
 
 def per_device(inputs, cotangent, gate_weight, up_weight, down_weight):
@@ -460,8 +511,8 @@
         vmem((3, 2, pad, half), BF16),
         vmem((3, 2, pad, half), BF16),
         vmem((hidden // 2, width), BF16),
-        pltpu.SemaphoreType.DMA((COPIES,)),
-        pltpu.SemaphoreType.DMA((COPIES,)),
+        pltpu.SemaphoreType.DMA((3,)),
+        pltpu.SemaphoreType.DMA((GROUPS,)),
         pltpu.SemaphoreType.DMA((5,)),
     ]
     return pl.pallas_call(

time: 78.5 us -> 74.8 us (0.953)
  Pallas kernels: 75.3 us -> 71.6 us
    pallas_call x1, Pallas kernels: 75.3 us -> 71.6 us  [per_device(): pl.pallas_call(kernel, out_shape=(jax.ShapeDtypeStruct((rows, half), BF16...]
where the time goes in v4:
time: 74.8 us; the launch traced here: 74.7 us
  Pallas kernels  71.6 us (96%)
  local copies, waits for them, and re-layouts  2.4 us (3%)
    pallas_call x1, Pallas kernels, per_device(): pl.pallas_call(kernel, out_shape=(jax.ShapeDtypeStruct((rows, half), BF16...  71.6 us
    unnamed x4, local copies, waits for them, and re-layouts  2.4 us

profile of v4, /device:TPU:0, one launch (start us, length us, event | category | flops | bytes accessed | tf_op | source)
XLA Modules:
  0.0 74.7 jit_solution(14403863165393846011)
XLA Ops:
  0.6 71.6 %swiglu_grads.1 = (bf16[128,896]{1,0:T(8,128)(2,1)}, bf16[74,1792]{1,0:T(8,128)(2,1)}) custom-call(bf16[128,896]{1,0:T(8,128)(2,1)} %x_ref.1, bf16[128,896]{1,0:T(8,128)(2,1)} %y_ref.1, bf16[74,1792]{1,0:T(8,128)(2,1)} %g_ref.1, bf16[74,1792]{1,0:T(8,128)(2,1)} %u_ref.1, bf16[74,1792]{1,0:T(8,128)(2,1)} %d_ref.1), custom_call_target="tpu_custom_call" | custom-call | tf_op jit(solution)/shard_map/swiglu_grads/pallas_call | solution.py:518
  72.3 0.0 copy-start
  72.3 1.7 %copy.9 = bf16[128,896]{1,0:T(8,128)(2,1)} copy(bf16[128,896]{1,0:T(8,128)(2,1)} %get-tuple-element.4) | data formatting | bytes 458752
  74.0 0.0 copy-done
  74.0 0.7 copy.10
Async XLA Ops:
  72.3 1.7 %copy-start = (bf16[74,1792]{1,0:T(8,128)(2,1)S(1)}, bf16[74,1792]{1,0:T(8,128)(2,1)}, u32[]{:S(2)}) copy-start(bf16[74,1792]{1,0:T(8,128)(2,1)} %get-tuple-element.5) | copy-start | bytes 795652

commit v5 on v4

--- a/solution.py
+++ b/solution.py
@@ -15,7 +15,7 @@
 BF16 = jnp.bfloat16
 N = 4
 GROUPS = 58
-VMEM_LIMIT = 66400000
+VMEM_LIMIT = 65000000
 SLOT = (0, 1, 3, 2)
 
 
@@ -305,12 +305,15 @@
 
     def forward(k, count):
         a = spot(k)
+        pl.delay(1)
         tokens = xb[a : a + count].reshape(count * block, width)
         both = dot(tokens, wb[0:2].reshape(2 * hidden, width), (1, 1))
         gu[a : a + count] = both.reshape(count, block, 2 * hidden)
+        pl.delay(1)
 
     def backward(k):
         a = spot(k)
+        pl.delay(1)
         dh = dot(yb[a].reshape(block, width), wb[2], (1, 1))
         g = gu[a, :, 0:hidden]
         sig = jax.nn.sigmoid(g)
@@ -320,6 +323,7 @@
         part = dot(dgu[...], wb[0:2].reshape(2 * hidden, width), (1, 0))
         dx[a] = part.reshape(2, rows, width)
         dgate[:, a * block : (a + 1) * block] = dgu[:, 0:hidden].T
+        pl.delay(1)
 
     def z_part(k, d, start):
         high, low = place.at_z(d)
@@ -357,11 +361,6 @@
     like_w = (wb.at[0, 0:pad], wb.at[0, 0 : 2 * pad])
     w1 = Scatter(links, place, "y", dw_part, ws, wr, like_w)
     order = (2, 1, 3, 0)
-
-    def b1_start(k):
-        b1[k % N].first()
-        b1[k % N].direct_right()
-        b1[k % N].direct_left()
 
     def end(stage, out, k):
         for h, total in enumerate(stage[k % N].totals()):
@@ -407,23 +406,27 @@
     for j in order:
         a1[j].direct_left()
         a1[j].direct_right()
-    b1_start(-1)
-    b1_start(1)
+    for k in (3, 1):
+        b1[k].first()
+    for k in (3, 1):
+        b1[k].direct_right()
+        b1[k].direct_left()
     ty.after_f2(0)
-    backward(0)
-    b1[0].first()
     tx.after_f2(0)
     tx.after_f2(-1)
     tx.after_f2(1)
     tx.after_f2(2)
     forward(2, 1)
-    b1[N - 1].second()
     ty.after2_rest()
     ty.after_f2(2)
     backward(2)
     for j in order:
         a1[j].first()
     b1[2].first()
+    b1[2].direct_right()
+    b1[2].direct_left()
+    backward(0)
+    b1[3].second()
     b1[1].second()
 
     whole = xb[...].reshape(N * block, width)
@@ -431,44 +434,54 @@
     upper = slice(other // 2, other)
     lower = slice(0, other // 2)
     crossings = []
-    for part in (upper, lower):
+
+    def other_rows(part):
+        pl.delay(1)
         wcs[part] = dot(dgate[other + part.start : other + part.stop], whole, (1, 0)).astype(BF16)
         crossings.append(links.group())
         links.copy(wcs.at[part], dwr.at[part], place.to("c", 1), crossings[-1], (1,))
-    b1[2].direct_right()
-    b1[2].direct_left()
-    dwf[upper] = dot(dgate[upper], whole, (1, 0))
+        pl.delay(1)
+
+    def own_rows(part):
+        pl.delay(1)
+        dwf[part] = dot(dgate[part], whole, (1, 0))
+        pl.delay(1)
+
+    other_rows(upper)
     b1[2].second()
+    a1[2].second()
+    other_rows(lower)
+    a1[1].second()
+    a1[3].second()
+    own_rows(upper)
     crossings[0].wait(dwr.at[upper])
     w1.first()
-    dwf[lower] = dot(dgate[lower], whole, (1, 0))
-    a1[2].second()
-    a1[1].second()
-    a1[3].second()
     a1[0].second()
+    b1[0].first()
+    own_rows(lower)
     end(b1, rb, 2)
     b2.first()
     crossings[1].wait(dwr.at[lower])
     w1.direct_right()
     w1.direct_left()
-    b1[0].second()
-    b1[0].direct_right()
-    b1[0].direct_left()
+    end(a1, ra, 2)
+    a2.first()
     end(b1, rb, 3)
     b2.direct_left()
     end(b1, rb, 1)
     b2.direct_right()
-    w1.second()
-    end(a1, ra, 2)
-    a2.first()
     end(a1, ra, 1)
     a2.direct_right()
     end(a1, ra, 3)
     a2.direct_left()
+    b1[0].second()
+    b1[0].direct_right()
+    b1[0].direct_left()
+    w1.second()
     b2.second()
-    end(b1, rb, 0)
     a2.second()
     end(a1, ra, 0)
+    end(b1, rb, 0)
     for h, total in enumerate(b2.totals()):
         dx_out[quarters(2 + h), :] = total.astype(BF16)
     for h, total in enumerate(a2.totals()):
@@ -518,8 +531,8 @@
     return pl.pallas_call(
         kernel,
         out_shape=(
-            jax.ShapeDtypeStruct((rows, half), BF16),
-            jax.ShapeDtypeStruct((units, width), BF16),
+            vmem((rows, half), BF16),
+            vmem((units, width), BF16),
         ),
         in_specs=[pl.BlockSpec(memory_space=pltpu.HBM)] * 5,
         out_specs=(pl.BlockSpec(memory_space=vmem),) * 2,

time: 74.8 us -> 70.1 us (0.937)
  Pallas kernels: 71.6 us -> 67.9 us
  local copies, waits for them, and re-layouts: 2.4 us -> 1.4 us
    pallas_call x1, Pallas kernels: 71.6 us -> 67.9 us  [per_device(): pl.pallas_call(kernel, out_shape=(vmem((rows, half), BF16), vmem((units,...]
    unnamed x4 -> x2, local copies, waits for them, and re-layouts: 2.4 us -> 1.4 us
where the time goes in v5:
time: 70.1 us; the launch traced here: 70 us
  Pallas kernels  67.9 us (97%)
  local copies, waits for them, and re-layouts  1.4 us (2%)
    pallas_call x1, Pallas kernels, per_device(): pl.pallas_call(kernel, out_shape=(vmem((rows, half), BF16), vmem((units,...  67.9 us

profile of v5, /device:TPU:0, one launch (start us, length us, event | category | flops | bytes accessed | tf_op | source)
XLA Modules:
  0.0 70.0 jit_solution(16888528884766514641)
XLA Ops:
  0.6 67.9 %swiglu_grads.1 = (bf16[128,896]{1,0:T(8,128)(2,1)S(1)}, bf16[74,1792]{1,0:T(8,128)(2,1)S(1)}) custom-call(bf16[128,896]{1,0:T(8,128)(2,1)} %x_ref.1, bf16[128,896]{1,0:T(8,128)(2,1)} %y_ref.1, bf16[74,1792]{1,0:T(8,128)(2,1)} %g_ref.1, bf16[74,1792]{1,0:T(8,128)(2,1)} %u_ref.1, bf16[74,1792]{1,0:T(8,128)(2,1)} %d_ref.1), custom_call_target="tpu_custom_call" | custom-call | tf_op jit(solution)/shard_map/swiglu_grads/pallas_call | solution.py:531
  68.6 0.7 copy.9
  69.3 0.7 %copy.10 = bf16[74,1792]{1,0:T(8,128)(2,1)} copy(bf16[74,1792]{1,0:T(8,128)(2,1)S(1)} %get-tuple-element.3) | data formatting | bytes 530432

commit v6 on v5

--- a/solution.py
+++ b/solution.py
@@ -448,17 +448,17 @@
         pl.delay(1)
 
     other_rows(upper)
+    own_rows(upper)
     b1[2].second()
     a1[2].second()
+    a1[1].second()
+    b1[0].first()
     other_rows(lower)
-    a1[1].second()
-    a1[3].second()
-    own_rows(upper)
     crossings[0].wait(dwr.at[upper])
     w1.first()
+    a1[3].second()
+    own_rows(lower)
     a1[0].second()
-    b1[0].first()
-    own_rows(lower)
     end(b1, rb, 2)
     b2.first()
     crossings[1].wait(dwr.at[lower])
@@ -466,17 +466,17 @@
     w1.direct_left()
     end(a1, ra, 2)
     a2.first()
+    b1[0].second()
+    b1[0].direct_right()
+    b1[0].direct_left()
     end(b1, rb, 3)
-    b2.direct_left()
     end(b1, rb, 1)
-    b2.direct_right()
     end(a1, ra, 1)
     a2.direct_right()
     end(a1, ra, 3)
     a2.direct_left()
-    b1[0].second()
-    b1[0].direct_right()
-    b1[0].direct_left()
+    b2.direct_left()
+    b2.direct_right()
     w1.second()
     b2.second()
     a2.second()

time: 70.1 us -> 70.3 us (level)
  no operation moved by 1% of the time
where the time goes in v6:
time: 70.3 us; the launch traced here: 70 us
  Pallas kernels  67.9 us (97%)
  local copies, waits for them, and re-layouts  1.4 us (2%)
    pallas_call x1, Pallas kernels, per_device(): pl.pallas_call(kernel, out_shape=(vmem((rows, half), BF16), vmem((units,...  67.9 us

profile of v6, /device:TPU:0, one launch (start us, length us, event | category | flops | bytes accessed | tf_op | source)
XLA Modules:
  0.0 70.0 jit_solution(479039441928061938)
XLA Ops:
  0.6 67.9 %swiglu_grads.1 = (bf16[128,896]{1,0:T(8,128)(2,1)S(1)}, bf16[74,1792]{1,0:T(8,128)(2,1)S(1)}) custom-call(bf16[128,896]{1,0:T(8,128)(2,1)} %x_ref.1, bf16[128,896]{1,0:T(8,128)(2,1)} %y_ref.1, bf16[74,1792]{1,0:T(8,128)(2,1)} %g_ref.1, bf16[74,1792]{1,0:T(8,128)(2,1)} %u_ref.1, bf16[74,1792]{1,0:T(8,128)(2,1)} %d_ref.1), custom_call_target="tpu_custom_call" | custom-call | tf_op jit(solution)/shard_map/swiglu_grads/pallas_call | solution.py:531
  68.6 0.7 copy.9
  69.2 0.7 %copy.10 = bf16[74,1792]{1,0:T(8,128)(2,1)} copy(bf16[74,1792]{1,0:T(8,128)(2,1)S(1)} %get-tuple-element.3) | data formatting | bytes 530432

commit v7 on v6

--- a/solution.py
+++ b/solution.py
@@ -458,9 +458,9 @@
     w1.first()
     a1[3].second()
     own_rows(lower)
-    a1[0].second()
     end(b1, rb, 2)
     b2.first()
+    a1[0].second()
     crossings[1].wait(dwr.at[lower])
     w1.direct_right()
     w1.direct_left()

time: 70.3 us -> 70.3 us (level)
  no operation moved by 1% of the time
where the time goes in v7:
time: 70.3 us; the launch traced here: 70 us
  Pallas kernels  67.9 us (97%)
  local copies, waits for them, and re-layouts  1.4 us (2%)
    pallas_call x1, Pallas kernels, per_device(): pl.pallas_call(kernel, out_shape=(vmem((rows, half), BF16), vmem((units,...  67.9 us

profile of v7, /device:TPU:0, one launch (start us, length us, event | category | flops | bytes accessed | tf_op | source)
XLA Modules:
  0.0 70.0 jit_solution(4767999870976725767)
XLA Ops:
  0.6 67.9 %swiglu_grads.1 = (bf16[128,896]{1,0:T(8,128)(2,1)S(1)}, bf16[74,1792]{1,0:T(8,128)(2,1)S(1)}) custom-call(bf16[128,896]{1,0:T(8,128)(2,1)} %x_ref.1, bf16[128,896]{1,0:T(8,128)(2,1)} %y_ref.1, bf16[74,1792]{1,0:T(8,128)(2,1)} %g_ref.1, bf16[74,1792]{1,0:T(8,128)(2,1)} %u_ref.1, bf16[74,1792]{1,0:T(8,128)(2,1)} %d_ref.1), custom_call_target="tpu_custom_call" | custom-call | tf_op jit(solution)/shard_map/swiglu_grads/pallas_call | solution.py:531
  68.6 0.7 copy.9
  69.2 0.7 %copy.10 = bf16[74,1792]{1,0:T(8,128)(2,1)} copy(bf16[74,1792]{1,0:T(8,128)(2,1)S(1)} %get-tuple-element.3) | data formatting | bytes 530432
